TPU v7x, 768 devices: a whole 4x8x12 slice. The times are simulated.
768 devices in a mesh: slab: 192 (over z, y, core), tile: 4 (over x).
Axes of the slice: x: 4, y: 8, z: 12, core: 2. Of those that a mesh axis runs over, the one named last changes fastest.
Arguments:
- load_field: float32 [3072, 16, 256], P(('slab', 'tile')), may hold values from -6 to 6
- orders: int32 [3072], P(('slab', 'tile')), may hold values from 7 to 15
- stiffness: float32 [3072, 768], P(('slab', 'tile')), may hold values from -1 to 5, as said below
- basis_table: float32 [3072, 768], P(('slab', 'tile')), may hold values from -0.25 to 1.25
- eigen_values: float32 [3072, 48], P(('slab', 'tile')), may hold values from 0.3 to 6
- route_plan: int32 [3072], P(('slab', 'tile')), may hold values from 0 to 3071, as said below
Outputs:
- solution: float32 [3072, 16, 256], P(('slab', 'tile'))
- residual: float32 [3072, 16, 256], P(('slab', 'tile'))
Inputs may be any that keep to these rules, and one draw needn't show every extreme that they name: `route_plan`: A permutation of all element indices. The element of the device at slab index p and tile index t with value v goes to the device at slab index (p + g) mod the slab axis's size and tile index t, where g = (v mod 4) // 1 is below 4; v = (that device's index) * 4 + (v mod 4). Every device's 4 slots are used, 1 by each of the devices 0 to 3 slab steps behind it. `stiffness`: three symmetric matrices per element with positive diagonals.
All inputs are finite; a program needn't handle non-finite values.
Results may differ from a plain program's by a relative error of at most 0.0003.
Values sent between devices are 32-bit elements; how exact they have to be, the bound alone decides.
No kernel may reach another device: no remote copies, remote signals or barrier semaphores. Data moves between devices by JAX's collectives and lax.ppermute only.
A program may use at most 32 MiB of HBM per device.

v0:
```python
import jax
import jax.numpy as jnp
from jax import lax
from jax.experimental import pallas as pl
from jax.experimental.pallas import tpu as pltpu
from jax.sharding import PartitionSpec as P

F32 = jnp.float32
BF16 = jnp.bfloat16
NB = 16
PL = 256
CHEB_LOW, CHEB_HIGH = 0.4, 8.0
CENTER = (CHEB_HIGH + CHEB_LOW) / 2.0
HALF = (CHEB_HIGH - CHEB_LOW) / 2.0
SIGMA = CENTER / HALF
RATIO = 1.0 / SIGMA
RATIO_NEXT = 1.0 / (2.0 * SIGMA - RATIO)
STEPS = (
    (0.0, 1.0 / CENTER),
    (RATIO_NEXT * RATIO, 2.0 * RATIO_NEXT / HALF),
) * 2

G_LOAD, G_STIFF, G_BASIS, G_EIG, G_FACE, G_ROWS = 0, 64, 82, 94, 100, 104
C_ACT, C_WGT, C_RD, C_KX, C_FACT, C_GACT, C_FW, C_GW, C_KGG, C_ROWS = (
    0, 256, 512, 768, 896, 904, 912, 920, 928, 936,
)
S_R, S_U, S_X, S_MF, S_GU, S_ROWS = 0, 256, 512, 768, 776, 784


def iota(shape, dim):
    return lax.broadcasted_iota(jnp.int32, shape, dim)


def split(value):
    high = value.astype(BF16)
    low = (value - high.astype(F32)).astype(BF16)
    return high, low


def dot(a, b):
    return jnp.dot(a, b, preferred_element_type=F32)


def blk(n, base=0, size=NB):
    if isinstance(n, int):
        return slice(base + n * size, base + (n + 1) * size)
    return pl.ds(pl.multiple_of(base + n * size, 8), size)


def loop(count, body, unroll):
    def step(i, carry):
        for k in range(unroll):
            body(i * unroll + k)
        return carry

    lax.fori_loop(0, count // unroll, step, 0)


def apply_weights(value, w_ref, n):
    rows = value.shape[0]
    high, low = split(value)
    both = dot(jnp.concatenate([high, low], axis=0), w_ref[blk(2 * n, 0, PL), :])
    return both[:rows] + both[rows:] + dot(high, w_ref[blk(2 * n + 1, 0, PL), :])


def apply_blocks(bd_ref, which, value, t):
    high, low = split(value)
    m_high = bd_ref[which * 512 + t * 64 : which * 512 + (t + 1) * 64, :64]
    m_low = bd_ref[which * 512 + 256 + t * 64 : which * 512 + 256 + (t + 1) * 64, :64]
    both = dot(jnp.concatenate([m_high, m_low], axis=0), high)
    return both[:64] + both[64:] + dot(m_high, low)


def face_stage(value, mask):
    low, high = value[:, :128], value[:, 128:]
    row = iota((8, 128), 0)
    lane = iota((8, 128), 1)
    before = jnp.where(row % 4 == 0, 0.0, pltpu.roll(high, 1, 0))
    after = jnp.where(row % 4 == 3, 0.0, pltpu.roll(low, 7, 0))
    low = low + jnp.where(lane < 16, pltpu.roll(before, 16, 1), 0.0)
    high = high + jnp.where(lane >= 112, pltpu.roll(after, 112, 1), 0.0)
    return jnp.concatenate([low, high], axis=1) * mask


def assemble(v_ref, ext_ref, xp_ref, c_ref, out):
    row = iota((NB, PL), 0)
    lane = iota((NB, 128), 1)

    def x_stage(t):
        for e in range(4):
            n = t * 4 + e
            m = v_ref[blk(n), :]
            if e > 0:
                left = v_ref[pl.ds(n * NB - 1, 1), :]
            else:
                left = ext_ref[pl.ds(t, 1), :]
            if e < 3:
                right = v_ref[pl.ds(n * NB + NB, 1), :]
            else:
                right = ext_ref[pl.ds(4 + t, 1), :]
            total = m + jnp.where(row == 0, left, 0.0) + jnp.where(row == NB - 1, right, 0.0)
            xp_ref[blk(n + 4), :] = total * c_ref[blk(n, C_ACT), :]

    def y_stage(t):
        for e in range(4):
            n = t * 4 + e
            x = xp_ref[blk(n + 4), :]
            before = xp_ref[blk(n), 128:]
            after = xp_ref[blk(n + 8), :128]
            low = x[:, :128] + jnp.where(lane < 16, pltpu.roll(before, 16, 1), 0.0)
            high = x[:, 128:] + jnp.where(lane >= 112, pltpu.roll(after, 112, 1), 0.0)
            z = jnp.concatenate([low, high], axis=1) * c_ref[blk(n, C_ACT), :]
            out(n, z)

    for t in range(4):
        x_stage(t)
    for t in range(4):
        y_stage(t)


def zero_borders(xp_ref):
    xp_ref[0:64, :] = jnp.zeros((64, PL), F32)
    xp_ref[320:384, :] = jnp.zeros((64, PL), F32)


def phase_one(step, c_ref, bd_ref, wf_ref, wb_ref, s_in, s_out, v_ref, v2_ref, xp_ref, ext_ref,
              sm_ref, a_ref, b_ref):
    alpha, beta = step

    def forward(n):
        rows = blk(n)
        value = c_ref[blk(n, C_WGT), :] * s_out[blk(n, S_R), :]
        v2_ref[rows, :] = apply_weights(value, wf_ref, n)

    loop(16, forward, 8)
    for t in range(4):
        h = apply_blocks(bd_ref, 0, v2_ref[t * 64 : t * 64 + 64, :], t)
        h = h * c_ref[C_RD + t * 64 : C_RD + t * 64 + 64, :]
        v2_ref[t * 64 : t * 64 + 64, :] = apply_blocks(bd_ref, 1, h, t)

    def backward(n):
        v_ref[blk(n), :] = c_ref[blk(n, C_ACT), :] * apply_weights(v2_ref[blk(n), :], wb_ref, n)

    loop(16, backward, 8)
    ext_ref[...] = jnp.zeros((8, PL), F32)

    def update(n, z):
        new = beta * (c_ref[blk(n, C_WGT), :] * z)
        if alpha != 0.0:
            new = new + alpha * s_in[blk(n, S_U), :]
        s_out[blk(n, S_U), :] = new

    assemble(v_ref, ext_ref, xp_ref, c_ref, update)
    faces = [v_ref[t * 64 : t * 64 + 1, :] for t in range(4)]
    faces += [v_ref[t * 64 + 63 : t * 64 + 64, :] for t in range(4)]
    faces = jnp.concatenate(faces, axis=0)
    s_out[S_MF : S_MF + 8, :] = faces
    inner = []
    for side in range(2):
        for t in range(4):
            n = t * 4 + 3 * side
            k = c_ref[blk(side * 4 + t, C_KX), :]
            inner.append(jnp.sum(k * s_out[blk(n, S_U), :], axis=0, keepdims=True))
    inner = jnp.concatenate(inner, axis=0)
    to_left = jnp.concatenate([faces[:4], inner[:4]], axis=0)
    to_right = jnp.concatenate([faces[4:], inner[4:]], axis=0)
    even = jnp.full((8, PL), sm_ref[0], jnp.int32) == 0
    a_ref[...] = jnp.where(even, to_right, to_left)
    b_ref[...] = jnp.where(even, to_left, to_right)


def phase_two(step, c_ref, bd_ref, m_ref, s_in, s_out, v_ref, v2_ref, xp_ref, ext_ref, sm_ref,
              a_ref, b_ref):
    alpha, beta = step
    even = jnp.full((8, PL), sm_ref[0], jnp.int32) == 0
    rec_a, rec_b = a_ref[...], b_ref[...]
    from_left = jnp.where(even, rec_b, rec_a)
    from_right = jnp.where(even, rec_a, rec_b)
    outer = jnp.concatenate([from_left[:4], from_right[:4]], axis=0)
    inner = jnp.concatenate([from_left[4:], from_right[4:]], axis=0)
    fact = c_ref[C_FACT : C_FACT + 8, :]
    gact = c_ref[C_GACT : C_GACT + 8, :]
    delta = beta * (c_ref[C_FW : C_FW + 8, :] * face_stage(fact * outer, fact))
    ghost = (outer + s_in[S_MF : S_MF + 8, :]) * gact
    ghost = beta * (c_ref[C_GW : C_GW + 8, :] * face_stage(ghost, gact))
    if alpha != 0.0:
        ghost = ghost + alpha * s_in[S_GU : S_GU + 8, :]
    s_out[S_GU : S_GU + 8, :] = ghost
    row = iota((NB, PL), 0)
    for t in range(4):
        for e in range(4):
            n = t * 4 + e
            u = s_in[blk(n, S_U), :]
            if e == 0:
                u = u + jnp.where(row == 0, delta[t : t + 1], 0.0)
            if e == 3:
                u = u + jnp.where(row == NB - 1, delta[4 + t : 5 + t], 0.0)
            s_out[blk(n, S_U), :] = u
            s_out[blk(n, S_X), :] = s_in[blk(n, S_X), :] + u

    for t in range(4):
        v2_ref[t * 64 : t * 64 + 64, :] = apply_blocks(
            bd_ref, 2, s_out[S_U + t * 64 : S_U + t * 64 + 64, :], t
        )
    high, low = split(ghost)
    both = jnp.concatenate([high, low], axis=0)
    row8 = iota((8, PL), 0)
    image = inner + c_ref[C_KGG : C_KGG + 8, :] * ghost
    for s in range(8):
        w = 16 + s
        part = dot(both, m_ref[blk(2 * w, 0, PL), :])
        part = part[:8] + part[8:] + dot(high, m_ref[blk(2 * w + 1, 0, PL), :])
        image = image + jnp.where(row8 == s, part, 0.0)
    ext_ref[...] = image * gact

    def local(n):
        rows = blk(n)
        q = v2_ref[rows, :] + apply_weights(s_out[blk(n, S_U), :], m_ref, n)
        v_ref[rows, :] = c_ref[blk(n, C_ACT), :] * q

    loop(16, local, 8)

    def update(n, z):
        s_out[blk(n, S_R), :] = s_in[blk(n, S_R), :] - z

    assemble(v_ref, ext_ref, xp_ref, c_ref, update)


def first_kernel(sm_ref, g_ref, c_ref, bd_ref, wf_ref, wb_ref, m_ref, s_ref, a_ref, b_ref,
                 v_ref, v2_ref, xp_ref, ext_ref, p_ref, ta_ref, tb_ref):
    zero_borders(xp_ref)
    row = iota((NB, PL), 0)
    lane = iota((NB, PL), 1)
    by_row = lane // NB == row
    by_col = lane % NB == row
    big_l = iota((PL, PL), 0)
    big_m = iota((PL, PL), 1)

    def hot(condition):
        return jnp.where(condition, 1.0, 0.0).astype(BF16)

    def expand(rows, mask, onehot):
        for i, (t, r) in enumerate(rows):
            p_ref[blk(i), :] = jnp.where(mask, g_ref[t, r : r + 1, :], 0.0)
        size = len(rows) * NB
        for start in range(0, size, 128):
            high, low = split(p_ref[start : start + 128, :])
            yield start, dot(high, onehot) + dot(low, onehot)

    own = [(t, e) for t in range(4) for e in range(4)]
    wide = own + [(t, 4) for t in range(4)] + [(t, 5) for t in range(4)]

    def basis(d):
        return [(t, G_BASIS + 3 * e + d) for t, e in own]

    def stiff(d, which):
        return [(t, G_STIFF + 3 * e + d) for t, e in which]

    e1 = hot(big_l % NB == big_m // NB)
    e2 = hot(big_l % NB == big_m % NB)
    e3 = hot(big_l // NB == big_m // NB)
    e4 = hot(big_l // NB == big_m % NB)
    block = (iota((128, PL), 0) // NB) % 4 == iota((128, PL), 1) // NB
    for which, (rows, mask, onehot) in enumerate(
        ((basis(0), by_col, e4), (basis(0), by_row, e2), (stiff(0, own), by_row, e2))
    ):
        for start, part in expand(rows, mask, onehot):
            high, low = split(jnp.where(block, part, 0.0))
            bd_ref[which * 512 + start : which * 512 + start + 128, :] = high
            bd_ref[which * 512 + 256 + start : which * 512 + 256 + start + 128, :] = low

    eig = jnp.concatenate([g_ref[t, G_EIG + e : G_EIG + e + 1, :] for t, e in wide], axis=0)
    high, low = split(eig)
    orders = dot(high, hot(big_l == 48))
    cross_hot = hot(big_l == 16 + big_m // NB) + hot(big_l == 32 + big_m % NB)
    cross = dot(high, cross_hot) + dot(low, cross_hot)
    for start, part in expand([(t, G_EIG + e) for t, e in own], lane == row, hot(big_l < 16)):
        v_ref[start : start + 128, :] = part
    for n in range(16):
        order = orders[n : n + 1, :]

        def along(index):
            return jnp.where((index.astype(F32) < order) | (index == NB - 1), 1.0, 0.0)

        c_ref[blk(n, C_ACT), :] = along(row) * (along(lane // NB) * along(lane % NB))
        c_ref[blk(n, C_RD), :] = 1.0 / (v_ref[blk(n), :] + cross[n : n + 1, :])
    order = orders[16:24, :]
    lane8 = iota((8, PL), 1)
    row8 = iota((8, PL), 0)

    def along8(index):
        return jnp.where((index.astype(F32) < order) | (index == NB - 1), 1.0, 0.0)

    gact = jnp.where(order > 0.0, along8(lane8 // NB) * along8(lane8 % NB), 0.0)
    fact = jnp.concatenate(
        [c_ref[t * 64 : t * 64 + 1, :] for t in range(4)]
        + [c_ref[t * 64 + 63 : t * 64 + 64, :] for t in range(4)],
        axis=0,
    )
    c_ref[C_FACT : C_FACT + 8, :] = fact
    c_ref[C_GACT : C_GACT + 8, :] = gact
    ghost_shares = face_stage((gact + fact) * gact, gact)
    c_ref[C_GW : C_GW + 8, :] = gact / jnp.maximum(ghost_shares, 1.0)
    for side in range(2):
        for t in range(4):
            e = 3 * side
            kx = g_ref[t, G_STIFF + 3 * e : G_STIFF + 3 * e + 1, :]
            edge = NB - 1 if side else 0
            col = jnp.sum(
                jnp.where((lane == edge * NB + row) & (row != edge), kx, 0.0), axis=1, keepdims=True
            )
            c_ref[blk(side * 4 + t, C_KX), :] = jnp.broadcast_to(col, (NB, PL))
    kgx = jnp.concatenate(
        [g_ref[t, G_STIFF + 12 : G_STIFF + 13, :] for t in range(4)]
        + [g_ref[t, G_STIFF + 15 : G_STIFF + 16, :] for t in range(4)],
        axis=0,
    )
    pick = lane8 == jnp.where(row8 < 4, PL - 1, 0)
    kgg = jnp.sum(jnp.where(pick, kgx, 0.0), axis=1, keepdims=True)
    c_ref[C_KGG : C_KGG + 8, :] = jnp.broadcast_to(kgg, (8, PL))

    v_ref[...] = c_ref[C_ACT : C_ACT + 256, :]
    ext_ref[...] = gact

    def weigh(n, z):
        c_ref[blk(n, C_WGT), :] = c_ref[blk(n, C_ACT), :] / jnp.maximum(z, 1.0)

    assemble(v_ref, ext_ref, xp_ref, c_ref, weigh)
    c_ref[C_FW : C_FW + 8, :] = jnp.concatenate(
        [c_ref[C_WGT + t * 64 : C_WGT + t * 64 + 1, :] for t in range(4)]
        + [c_ref[C_WGT + t * 64 + 63 : C_WGT + t * 64 + 64, :] for t in range(4)],
        axis=0,
    )
    for t in range(4):
        v_ref[t * 64 : t * 64 + 64, :] = c_ref[t * 64 : t * 64 + 64, :] * g_ref[t, 0:64, :]
    ghost_load = jnp.concatenate(
        [g_ref[t, G_FACE : G_FACE + 1, :] for t in range(4)]
        + [g_ref[t, G_FACE + 1 : G_FACE + 2, :] for t in range(4)],
        axis=0,
    )
    ext_ref[...] = gact * ghost_load

    def start_residual(n, z):
        s_ref[blk(n, S_R), :] = z

    assemble(v_ref, ext_ref, xp_ref, c_ref, start_residual)
    s_ref[S_X : S_X + 256, :] = jnp.zeros((256, PL), F32)
    s_ref[S_GU : S_GU + 8, :] = jnp.zeros((8, PL), F32)

    def product(w_ref, mask, rows_y, hot_y, rows_z, hot_z):
        for start, part in expand(rows_y, mask, hot_y):
            ta_ref[start : start + 128, :] = part
        for start, part in expand(rows_z, mask, hot_z):
            tb_ref[start : start + 128, :] = part

        def build(n):
            ty = ta_ref[blk(n), :]
            tz = tb_ref[blk(n), :]
            for b in range(NB):
                high, low = split(ty[b : b + 1, :] * tz)
                w_ref[pl.ds(pl.multiple_of(n * 512 + b * NB, 16), NB), :] = high
                w_ref[pl.ds(pl.multiple_of(n * 512 + 256 + b * NB, 16), NB), :] = low

        loop(16, build, 2)

    product(wf_ref, by_row, basis(1), e1, basis(2), e2)
    product(wb_ref, by_col, basis(1), e3, basis(2), e4)

    for start, part in expand(stiff(1, wide), by_col, e3):
        ta_ref[start : start + 128, :] = part
    for start, part in expand(stiff(2, wide), by_col, e4):
        tb_ref[start : start + 128, :] = part

    def build_sum(n):
        ty = ta_ref[blk(n), :]
        tz = tb_ref[blk(n), :]
        for j in range(NB):
            value = jnp.where(by_col, ty[j : j + 1, :], 0.0)
            value = value + jnp.where(lane // NB == j, tz, 0.0)
            high, low = split(value)
            m_ref[pl.ds(pl.multiple_of(n * 512 + j * NB, 16), NB), :] = high
            m_ref[pl.ds(pl.multiple_of(n * 512 + 256 + j * NB, 16), NB), :] = low

    loop(24, build_sum, 2)
    phase_one(STEPS[0], c_ref, bd_ref, wf_ref, wb_ref, s_ref, s_ref, v_ref, v2_ref, xp_ref,
              ext_ref, sm_ref, a_ref, b_ref)


def middle_kernel(k, sm_ref, ra_ref, rb_ref, c_ref, bd_ref, wf_ref, wb_ref, m_ref, si_ref,
                  so_ref, a_ref, b_ref, v_ref, v2_ref, xp_ref, ext_ref):
    zero_borders(xp_ref)
    phase_two(STEPS[k], c_ref, bd_ref, m_ref, si_ref, so_ref, v_ref, v2_ref, xp_ref, ext_ref,
              sm_ref, ra_ref, rb_ref)
    phase_one(STEPS[k + 1], c_ref, bd_ref, wf_ref, wb_ref, so_ref, so_ref, v_ref, v2_ref, xp_ref,
              ext_ref, sm_ref, a_ref, b_ref)


def last_kernel(sm_ref, ra_ref, rb_ref, c_ref, bd_ref, m_ref, si_ref, x_ref, r_ref,
                so_ref, v_ref, v2_ref, xp_ref, ext_ref):
    zero_borders(xp_ref)
    phase_two(STEPS[3], c_ref, bd_ref, m_ref, si_ref, so_ref, v_ref, v2_ref, xp_ref, ext_ref,
              sm_ref, ra_ref, rb_ref)
    t = sm_ref[1]
    for e in range(4):
        x_ref[e * NB : (e + 1) * NB, :] = so_ref[pl.ds(pl.multiple_of(S_X + t * 64 + e * NB, 8), NB), :]
        r_ref[e * NB : (e + 1) * NB, :] = so_ref[pl.ds(pl.multiple_of(S_R + t * 64 + e * NB, 8), NB), :]


VM = pl.BlockSpec(memory_space=pltpu.VMEM)
SM = pl.BlockSpec(memory_space=pltpu.SMEM)


def struct(rows, dtype=F32):
    return jax.ShapeDtypeStruct((rows, PL), dtype)


WORK = [pltpu.VMEM((256, PL), F32), pltpu.VMEM((256, PL), F32), pltpu.VMEM((384, PL), F32),
        pltpu.VMEM((8, PL), F32)]
LIMIT = pltpu.CompilerParams(vmem_limit_bytes=12 * 2**20)


def call(kernel, name, ins, outs, scratch):
    return pl.pallas_call(
        kernel,
        name=name,
        in_specs=[SM] + [VM] * ins,
        out_specs=[VM] * len(outs),
        out_shape=outs,
        scratch_shapes=scratch,
        compiler_params=LIMIT,
    )


def per_device(load_field, orders, stiffness, basis_table, eigen_values, route_plan):
    slabs = lax.axis_size("slab")
    tiles = lax.axis_size("tile")
    p = lax.axis_index("slab")
    even = p % 2 == 0
    scalars = jnp.stack([p % 2, lax.axis_index("tile")]).astype(jnp.int32)
    swap_a = [(i, i ^ 1) for i in range(slabs)]
    swap_b = [(i, (i + 1) % slabs) if i % 2 else (i, (i - 1) % slabs) for i in range(slabs)]
    swap_in = [(i, j) for i, j in swap_b if abs(i - j) == 1]

    ord_f = orders.astype(F32)
    lane = jnp.arange(PL, dtype=jnp.int32)
    eig_rows = jnp.pad(eigen_values, ((0, 0), (0, PL - eigen_values.shape[1])))
    order_rows = jnp.where(lane[None, :] == 48, ord_f[:, None], 0.0)
    table = basis_table.reshape(4, 3, PL)
    stiff = stiffness.reshape(4, 3, PL)
    slots = jnp.concatenate([table, eig_rows[:, None, :]], axis=1)
    to_right = jnp.concatenate(
        [load_field[3, NB - 1 :, :], stiff[3], order_rows[3:4], jnp.zeros((3, PL), F32)], axis=0
    )
    to_left = jnp.concatenate(
        [load_field[0, :1, :], stiff[0], order_rows[0:1] + eig_rows[1:2], table[1]], axis=0
    )
    rec_a = lax.ppermute(jnp.where(even, to_right, to_left), "slab", swap_a)
    rec_b = lax.ppermute(jnp.where(even, to_left, to_right), "slab", swap_b)
    slot_2 = lax.ppermute(slots[2], "slab", [((i + 2) % slabs, i) for i in range(slabs)])
    slot_3 = lax.ppermute(slots[3], "slab", [((i + 3) % slabs, i) for i in range(slabs)])
    from_right = jnp.where(even, rec_a, rec_b)
    from_left = jnp.where(even, rec_b, rec_a)
    slot_1 = jnp.concatenate(
        [from_right[5:8], jnp.where(lane[None, :] < 48, from_right[4:5], 0.0)], axis=0
    )
    from_left = jnp.where(p == 0, 0.0, from_left)
    from_right = jnp.where(p == slabs - 1, 0.0, from_right)
    which = (route_plan % 4)[:, None, None]
    home = jnp.where(
        which == 0,
        slots[0][None],
        jnp.where(which == 1, slot_1[None], jnp.where(which == 2, slot_2[None], slot_3[None])),
    )
    only_order = lane[None, :] == 48
    block = jnp.concatenate(
        [
            load_field.reshape(64, PL),
            stiff.reshape(12, PL),
            from_left[1:4],
            from_right[1:4],
            home[:, :3].reshape(12, PL),
            home[:, 3] + order_rows,
            jnp.where(only_order, from_left[4:5], 0.0),
            jnp.where(only_order, from_right[4:5], 0.0),
            from_left[0:1],
            from_right[0:1],
            jnp.zeros((2, PL), F32),
        ],
        axis=0,
    )
    gathered = lax.all_to_all(
        jnp.broadcast_to(block[None], (tiles, G_ROWS, PL)), "tile", 0, 0
    )

    state = struct(S_ROWS)
    message = struct(8)
    consts, blocks, w_f, w_b, w_m, s, a, b = call(
        first_kernel,
        "setup_and_solve",
        1,
        [struct(C_ROWS), struct(1536, BF16), struct(16 * 512, BF16), struct(16 * 512, BF16),
         struct(24 * 512, BF16), state, message, message],
        WORK + [pltpu.VMEM((384, PL), F32)] * 3,
    )(scalars, gathered)
    for k in range(3):
        ra = lax.ppermute(a, "slab", swap_a)
        rb = lax.ppermute(b, "slab", swap_in)

        def kernel(*refs, k=k):
            middle_kernel(k, *refs)

        s, a, b = call(kernel, "operator_and_solve_%d" % k, 8, [state, message, message], WORK)(
            scalars, ra, rb, consts, blocks, w_f, w_b, w_m, s
        )
    ra = lax.ppermute(a, "slab", swap_a)
    rb = lax.ppermute(b, "slab", swap_in)
    x, r = call(
        last_kernel, "last_operator", 6, [struct(64), struct(64)],
        [pltpu.VMEM((S_ROWS, PL), F32)] + WORK,
    )(scalars, ra, rb, consts, blocks, w_m, s)
    return x.reshape(load_field.shape), r.reshape(load_field.shape)


def solution(mesh):
    both = ("slab", "tile")
    in_specs = (P(both, None, None), P(both), P(both, None), P(both, None), P(both, None), P(both))
    out_specs = (P(both, None, None), P(both, None, None))
    return jax.shard_map(
        per_device, mesh=mesh, in_specs=in_specs, out_specs=out_specs, check_vma=False
    )
```

profile of v0, /device:TPU:512, one launch (start us, length us, event | category | flops | bytes accessed | tf_op | source)
XLA Modules:
  0.0 105.5 jit_solution(3461300129257128940)
XLA Ops:
  0.6 0.7 pad_bitcast_fusion
  1.3 0.8 pad_maximum_fusion.3
  2.2 6.8 %collective-permute-start.3 = (f32[4,256]{1,0:T(4,128)S(1)}, f32[4,256]{1,0:T(4,128)S(1)}, u32[]{:S(2)}, u32[]{:S(2)}) collective-permute-start(f32[4,256]{1,0:T(4,128)S(1)} %bitcast.28), channel_id=1, source_target_pairs={{12,0},{16,4},{20,8},{24,12},{28,16},{32,20},{36,24},{40,28},{44,3... | collective-permute-start | bytes 12296 | tf_op jit(solution)/shard_map/ppermute | solution.py:460
  9.0 3.3 %collective-permute-start.2 = (f32[4,256]{1,0:T(4,128)S(1)}, f32[4,256]{1,0:T(4,128)S(1)}, u32[]{:S(2)}, u32[]{:S(2)}) collective-permute-start(f32[4,256]{1,0:T(4,128)S(1)} %bitcast.29), channel_id=1, source_target_pairs={{8,0},{12,4},{16,8},{20,12},{24,16},{28,20},{32,24},{36,28},{40,32... | collective-permute-start | bytes 12296 | tf_op jit(solution)/shard_map/ppermute | solution.py:459
  12.3 0.7 slice_reduce_fusion.1
  13.0 0.7 convert_element_type.5
  13.7 0.7 slice_bitcast_fusion.2
  14.4 0.1 broadcast_select_fusion.2
  14.5 0.7 fusion.3
  15.2 0.8 slice_reduce_fusion.2
  16.0 0.1 pad.12.clone
  16.1 0.1 fusion
  16.1 1.9 %collective-permute-start.1 = (f32[8,256]{1,0:T(8,128)S(1)}, f32[8,256]{1,0:T(8,128)S(1)}, u32[]{:S(2)}, u32[]{:S(2)}) collective-permute-start(f32[8,256]{1,0:T(8,128)S(1)} %get-tuple-element.48), channel_id=1, source_target_pairs={{0,4},{4,0},{8,12},{12,8},{16,20},{20,16},{24,28},{28,24},{32,36},... | collective-permute-start | bytes 24584 | tf_op jit(solution)/shard_map/ppermute | solution.py:457
  18.1 3.4 %collective-permute-start = (f32[8,256]{1,0:T(8,128)S(1)}, f32[8,256]{1,0:T(8,128)S(1)}, u32[]{:S(2)}, u32[]{:S(2)}) collective-permute-start(f32[8,256]{1,0:T(8,128)S(1)} %get-tuple-element.49), channel_id=1, source_target_pairs={{0,764},{4,8},{8,4},{12,16},{16,12},{20,24},{24,20},{28,32},{32,28... | collective-permute-start | bytes 24584 | tf_op jit(solution)/shard_map/ppermute | solution.py:458
  21.4 0.7 broadcast_compare_fusion.2
  22.1 0.7 reshape_reshape.3
  22.8 0.0 collective-permute-done.1
  22.8 3.5 %collective-permute-done = f32[8,256]{1,0:T(8,128)S(1)} collective-permute-done((f32[8,256]{1,0:T(8,128)S(1)}, f32[8,256]{1,0:T(8,128)S(1)}, u32[]{:S(2)}, u32[]{:S(2)}) %collective-permute-start) | collective-permute-done | bytes 8224 | tf_op jit(solution)/shard_map/ppermute | solution.py:458
  26.4 0.0 collective-permute-done.3
  26.4 0.0 collective-permute-done.2
  26.5 0.1 select_select_fusion
  26.5 0.1 fusion.2
  26.6 1.2 %concatenate.19 = f32[104,256]{1,0:T(8,128)S(1)} concatenate(f32[64,256]{1,0:T(8,128)} %bitcast.25, f32[12,256]{1,0:T(8,128)S(1)} %reshape_reshape.3, f32[3,256]{1,0:T(4,128)S(1)} %slice.89, f32[3,256]{1,0:T(4,128)S(1)} %slice.90, f32[12,256]{1,0:T(8,128)S(1)} %reshape.56, f32[4,256]{1,0:T(4,128)S(1)} %fusion.2, f32[1,256]{1,0:T(1,128)S(1)} %get-tuple-element.57, ...), dimensions={0} | concatenate | bytes 212992 | tf_op jit(solution)/shard_map/concatenate | solution.py:475
  27.8 0.8 broadcast_in_dim.122
  28.6 4.3 %all-to-all-start = ((f32[4,104,256]{2,1,0:T(8,128)}), f32[4,104,256]{2,1,0:T(8,128)S(1)}, u32[]{:S(2)}, u32[]{:S(2)}) async-start(f32[4,104,256]{2,1,0:T(8,128)} %broadcast_in_dim.122), calls=%async_computation | async-start | bytes 851968 | tf_op jit(solution)/shard_map/all_to_all | solution.py:491
  32.9 0.1 pad_add_fusion.sm_ref.refs_0_
  33.0 7.5 %all-to-all-done.g_ref = f32[4,104,256]{2,1,0:T(8,128)S(1)} async-done(((f32[4,104,256]{2,1,0:T(8,128)}), f32[4,104,256]{2,1,0:T(8,128)S(1)}, u32[]{:S(2)}, u32[]{:S(2)}) %all-to-all-start) | async-done | bytes 426016 | tf_op jit(solution)/shard_map/all_to_all | solution.py:491
  40.5 8.0 %setup_and_solve.1 = (f32[936,256]{1,0:T(8,128)S(1)}, bf16[1536,256]{1,0:T(8,128)(2,1)S(1)}, bf16[8192,256]{1,0:T(8,128)(2,1)S(1)}, bf16[8192,256]{1,0:T(8,128)(...) custom-call(s32[2]{0:T(128)S(1)} %pad_add_fusion.sm_ref.refs_0_, ...), custom_call_target="tpu_custom_call" | custom-call | tf_op jit(solution)/shard_map/setup_and_solve/pallas_call | solution.py:497
  48.5 1.9 %collective-permute-start.4 = (f32[8,256]{1,0:T(8,128)S(1)}, f32[8,256]{1,0:T(8,128)S(1)}, u32[]{:S(2)}, u32[]{:S(2)}) collective-permute-start(f32[8,256]{1,0:T(8,128)S(1)} %get-tuple-element.21), channel_id=1, source_target_pairs={{0,4},{4,0},{8,12},{12,8},{16,20},{20,16},{24,28},{28,24},{32,36},... | collective-permute-start | bytes 24584 | tf_op jit(solution)/shard_map/ppermute | solution.py:506
  50.5 1.9 %collective-permute-start.5 = (f32[8,256]{1,0:T(8,128)S(1)}, f32[8,256]{1,0:T(8,128)S(1)}, u32[]{:S(2)}, u32[]{:S(2)}) collective-permute-start(f32[8,256]{1,0:T(8,128)S(1)} %get-tuple-element.22), channel_id=1, source_target_pairs={{4,8},{8,4},{12,16},{16,12},{20,24},{24,20},{28,32},{32,28},{36,40... | collective-permute-start | bytes 24584 | tf_op jit(solution)/shard_map/ppermute | solution.py:507
  52.4 0.0 collective-permute-done.4.refs_1_
  52.4 6.3 %collective-permute-done.5.refs_2_ = f32[8,256]{1,0:T(8,128)S(1)} collective-permute-done((f32[8,256]{1,0:T(8,128)S(1)}, f32[8,256]{1,0:T(8,128)S(1)}, u32[]{:S(2)}, u32[]{:S(2)}) %collective-permute-start.5) | collective-permute-done | bytes 8224 | tf_op jit(solution)/shard_map/ppermute | solution.py:507
  58.8 4.5 %operator_and_solve_0.1 = (f32[784,256]{1,0:T(8,128)S(1)}, f32[8,256]{1,0:T(8,128)S(1)}, f32[8,256]{1,0:T(8,128)S(1)}) custom-call(s32[2]{0:T(128)S(1)} %pad_add_fusion.sm_ref.refs_0_, f32[8,256]{1,0:T(8,128)S(1)} %collective-permute-done.4.refs_1_, f32[8,256]{1,0:T(8,128)S(1)} %collective-permute-done.5.refs_2_, ...), custom_call_target="tpu_custom_call" | custom-call | tf_op jit(solution)/shard_map/operator_and_solve_0/pallas_call | solution.py:512
  63.2 1.9 %collective-permute-start.6 = (f32[8,256]{1,0:T(8,128)S(1)}, f32[8,256]{1,0:T(8,128)S(1)}, u32[]{:S(2)}, u32[]{:S(2)}) collective-permute-start(f32[8,256]{1,0:T(8,128)S(1)} %get-tuple-element.29), channel_id=1, source_target_pairs={{0,4},{4,0},{8,12},{12,8},{16,20},{20,16},{24,28},{28,24},{32,36},... | collective-permute-start | bytes 24584 | tf_op jit(solution)/shard_map/ppermute | solution.py:506
  65.1 1.9 %collective-permute-start.7 = (f32[8,256]{1,0:T(8,128)S(1)}, f32[8,256]{1,0:T(8,128)S(1)}, u32[]{:S(2)}, u32[]{:S(2)}) collective-permute-start(f32[8,256]{1,0:T(8,128)S(1)} %get-tuple-element.30), channel_id=1, source_target_pairs={{4,8},{8,4},{12,16},{16,12},{20,24},{24,20},{28,32},{32,28},{36,40... | collective-permute-start | bytes 24584 | tf_op jit(solution)/shard_map/ppermute | solution.py:507
  67.1 0.0 collective-permute-done.6.refs_1_
  67.1 6.3 %collective-permute-done.7.refs_2_ = f32[8,256]{1,0:T(8,128)S(1)} collective-permute-done((f32[8,256]{1,0:T(8,128)S(1)}, f32[8,256]{1,0:T(8,128)S(1)}, u32[]{:S(2)}, u32[]{:S(2)}) %collective-permute-start.7) | collective-permute-done | bytes 8224 | tf_op jit(solution)/shard_map/ppermute | solution.py:507
  73.4 4.4 %operator_and_solve_1.1 = (f32[784,256]{1,0:T(8,128)S(1)}, f32[8,256]{1,0:T(8,128)S(1)}, f32[8,256]{1,0:T(8,128)S(1)}) custom-call(s32[2]{0:T(128)S(1)} %pad_add_fusion.sm_ref.refs_0_, f32[8,256]{1,0:T(8,128)S(1)} %collective-permute-done.6.refs_1_, f32[8,256]{1,0:T(8,128)S(1)} %collective-permute-done.7.refs_2_, ...), custom_call_target="tpu_custom_call" | custom-call | tf_op jit(solution)/shard_map/operator_and_solve_1/pallas_call | solution.py:512
  77.9 1.9 %collective-permute-start.8 = (f32[8,256]{1,0:T(8,128)S(1)}, f32[8,256]{1,0:T(8,128)S(1)}, u32[]{:S(2)}, u32[]{:S(2)}) collective-permute-start(f32[8,256]{1,0:T(8,128)S(1)} %get-tuple-element.32), channel_id=1, source_target_pairs={{0,4},{4,0},{8,12},{12,8},{16,20},{20,16},{24,28},{28,24},{32,36},... | collective-permute-start | bytes 24584 | tf_op jit(solution)/shard_map/ppermute | solution.py:506
  79.8 1.9 %collective-permute-start.9 = (f32[8,256]{1,0:T(8,128)S(1)}, f32[8,256]{1,0:T(8,128)S(1)}, u32[]{:S(2)}, u32[]{:S(2)}) collective-permute-start(f32[8,256]{1,0:T(8,128)S(1)} %get-tuple-element.33), channel_id=1, source_target_pairs={{4,8},{8,4},{12,16},{16,12},{20,24},{24,20},{28,32},{32,28},{36,40... | collective-permute-start | bytes 24584 | tf_op jit(solution)/shard_map/ppermute | solution.py:507
  81.7 0.0 collective-permute-done.8.refs_1_
  81.7 6.3 %collective-permute-done.9.refs_2_ = f32[8,256]{1,0:T(8,128)S(1)} collective-permute-done((f32[8,256]{1,0:T(8,128)S(1)}, f32[8,256]{1,0:T(8,128)S(1)}, u32[]{:S(2)}, u32[]{:S(2)}) %collective-permute-start.9) | collective-permute-done | bytes 8224 | tf_op jit(solution)/shard_map/ppermute | solution.py:507
  88.1 4.5 %operator_and_solve_2.1 = (f32[784,256]{1,0:T(8,128)S(1)}, f32[8,256]{1,0:T(8,128)S(1)}, f32[8,256]{1,0:T(8,128)S(1)}) custom-call(s32[2]{0:T(128)S(1)} %pad_add_fusion.sm_ref.refs_0_, f32[8,256]{1,0:T(8,128)S(1)} %collective-permute-done.8.refs_1_, f32[8,256]{1,0:T(8,128)S(1)} %collective-permute-done.9.refs_2_, ...), custom_call_target="tpu_custom_call" | custom-call | tf_op jit(solution)/shard_map/operator_and_solve_2/pallas_call | solution.py:512
  92.6 1.9 %collective-permute-start.10 = (f32[8,256]{1,0:T(8,128)S(1)}, f32[8,256]{1,0:T(8,128)S(1)}, u32[]{:S(2)}, u32[]{:S(2)}) collective-permute-start(f32[8,256]{1,0:T(8,128)S(1)} %get-tuple-element.35), channel_id=1, source_target_pairs={{0,4},{4,0},{8,12},{12,8},{16,20},{20,16},{24,28},{28,24},{32,36},... | collective-permute-start | bytes 24584 | tf_op jit(solution)/shard_map/ppermute | solution.py:515
  94.5 1.9 %collective-permute-start.11 = (f32[8,256]{1,0:T(8,128)S(1)}, f32[8,256]{1,0:T(8,128)S(1)}, u32[]{:S(2)}, u32[]{:S(2)}) collective-permute-start(f32[8,256]{1,0:T(8,128)S(1)} %get-tuple-element.36), channel_id=1, source_target_pairs={{4,8},{8,4},{12,16},{16,12},{20,24},{24,20},{28,32},{32,28},{36,40... | collective-permute-start | bytes 24584 | tf_op jit(solution)/shard_map/ppermute | solution.py:516
  96.4 0.0 collective-permute-done.10.ra_ref
  96.4 6.3 %collective-permute-done.11.rb_ref = f32[8,256]{1,0:T(8,128)S(1)} collective-permute-done((f32[8,256]{1,0:T(8,128)S(1)}, f32[8,256]{1,0:T(8,128)S(1)}, u32[]{:S(2)}, u32[]{:S(2)}) %collective-permute-start.11) | collective-permute-done | bytes 8224 | tf_op jit(solution)/shard_map/ppermute | solution.py:516
  102.8 2.8 %last_operator.1 = (f32[64,256]{1,0:T(8,128)}, f32[64,256]{1,0:T(8,128)}) custom-call(s32[2]{0:T(128)S(1)} %pad_add_fusion.sm_ref.refs_0_, f32[8,256]{1,0:T(8,128)S(1)} %collective-permute-done.10.ra_ref, f32[8,256]{1,0:T(8,128)S(1)} %collective-permute-done.11.rb_ref, f32[936,256]{1,0:T(8,128)S(1)} %get-tuple-element.23.refs_3_.c_ref, ...), custom_call_target="tpu_custom_call" | custom-call | tf_op jit(solution)/shard_map/last_operator/pallas_call | solution.py:517
  (20 shorter events, 0.1 us)
Async XLA Ops:
  2.2 24.3 %collective-permute-start.3 = (f32[4,256]{1,0:T(4,128)S(1)}, f32[4,256]{1,0:T(4,128)S(1)}, u32[]{:S(2)}, u32[]{:S(2)}) collective-permute-start(f32[4,256]{1,0:T(4,128)S(1)} %bitcast.28), channel_id=1, source_target_pairs={{12,0},{16,4},{20,8},{24,12},{28,16},{32,20},{36,24},{40,28},{44,3... | collective-permute-start | bytes 12296 | tf_op jit(solution)/shard_map/ppermute | solution.py:460
  9.0 17.5 %collective-permute-start.2 = (f32[4,256]{1,0:T(4,128)S(1)}, f32[4,256]{1,0:T(4,128)S(1)}, u32[]{:S(2)}, u32[]{:S(2)}) collective-permute-start(f32[4,256]{1,0:T(4,128)S(1)} %bitcast.29), channel_id=1, source_target_pairs={{8,0},{12,4},{16,8},{20,12},{24,16},{28,20},{32,24},{36,28},{40,32... | collective-permute-start | bytes 12296 | tf_op jit(solution)/shard_map/ppermute | solution.py:459
  16.1 6.7 %collective-permute-start.1 = (f32[8,256]{1,0:T(8,128)S(1)}, f32[8,256]{1,0:T(8,128)S(1)}, u32[]{:S(2)}, u32[]{:S(2)}) collective-permute-start(f32[8,256]{1,0:T(8,128)S(1)} %get-tuple-element.48), channel_id=1, source_target_pairs={{0,4},{4,0},{8,12},{12,8},{16,20},{20,16},{24,28},{28,24},{32,36},... | collective-permute-start | bytes 24584 | tf_op jit(solution)/shard_map/ppermute | solution.py:457
  18.1 8.3 %collective-permute-start = (f32[8,256]{1,0:T(8,128)S(1)}, f32[8,256]{1,0:T(8,128)S(1)}, u32[]{:S(2)}, u32[]{:S(2)}) collective-permute-start(f32[8,256]{1,0:T(8,128)S(1)} %get-tuple-element.49), channel_id=1, source_target_pairs={{0,764},{4,8},{8,4},{12,16},{16,12},{20,24},{24,20},{28,32},{32,28... | collective-permute-start | bytes 24584 | tf_op jit(solution)/shard_map/ppermute | solution.py:458
  28.6 11.8 %all-to-all-start = ((f32[4,104,256]{2,1,0:T(8,128)}), f32[4,104,256]{2,1,0:T(8,128)S(1)}, u32[]{:S(2)}, u32[]{:S(2)}) async-start(f32[4,104,256]{2,1,0:T(8,128)} %broadcast_in_dim.122), calls=%async_computation | async-start | bytes 851968 | tf_op jit(solution)/shard_map/all_to_all | solution.py:491
  48.5 3.9 %collective-permute-start.4 = (f32[8,256]{1,0:T(8,128)S(1)}, f32[8,256]{1,0:T(8,128)S(1)}, u32[]{:S(2)}, u32[]{:S(2)}) collective-permute-start(f32[8,256]{1,0:T(8,128)S(1)} %get-tuple-element.21), channel_id=1, source_target_pairs={{0,4},{4,0},{8,12},{12,8},{16,20},{20,16},{24,28},{28,24},{32,36},... | collective-permute-start | bytes 24584 | tf_op jit(solution)/shard_map/ppermute | solution.py:506
  50.5 8.3 %collective-permute-start.5 = (f32[8,256]{1,0:T(8,128)S(1)}, f32[8,256]{1,0:T(8,128)S(1)}, u32[]{:S(2)}, u32[]{:S(2)}) collective-permute-start(f32[8,256]{1,0:T(8,128)S(1)} %get-tuple-element.22), channel_id=1, source_target_pairs={{4,8},{8,4},{12,16},{16,12},{20,24},{24,20},{28,32},{32,28},{36,40... | collective-permute-start | bytes 24584 | tf_op jit(solution)/shard_map/ppermute | solution.py:507
  63.2 3.9 %collective-permute-start.6 = (f32[8,256]{1,0:T(8,128)S(1)}, f32[8,256]{1,0:T(8,128)S(1)}, u32[]{:S(2)}, u32[]{:S(2)}) collective-permute-start(f32[8,256]{1,0:T(8,128)S(1)} %get-tuple-element.29), channel_id=1, source_target_pairs={{0,4},{4,0},{8,12},{12,8},{16,20},{20,16},{24,28},{28,24},{32,36},... | collective-permute-start | bytes 24584 | tf_op jit(solution)/shard_map/ppermute | solution.py:506
  65.1 8.3 %collective-permute-start.7 = (f32[8,256]{1,0:T(8,128)S(1)}, f32[8,256]{1,0:T(8,128)S(1)}, u32[]{:S(2)}, u32[]{:S(2)}) collective-permute-start(f32[8,256]{1,0:T(8,128)S(1)} %get-tuple-element.30), channel_id=1, source_target_pairs={{4,8},{8,4},{12,16},{16,12},{20,24},{24,20},{28,32},{32,28},{36,40... | collective-permute-start | bytes 24584 | tf_op jit(solution)/shard_map/ppermute | solution.py:507
  77.9 3.9 %collective-permute-start.8 = (f32[8,256]{1,0:T(8,128)S(1)}, f32[8,256]{1,0:T(8,128)S(1)}, u32[]{:S(2)}, u32[]{:S(2)}) collective-permute-start(f32[8,256]{1,0:T(8,128)S(1)} %get-tuple-element.32), channel_id=1, source_target_pairs={{0,4},{4,0},{8,12},{12,8},{16,20},{20,16},{24,28},{28,24},{32,36},... | collective-permute-start | bytes 24584 | tf_op jit(solution)/shard_map/ppermute | solution.py:506
  79.8 8.3 %collective-permute-start.9 = (f32[8,256]{1,0:T(8,128)S(1)}, f32[8,256]{1,0:T(8,128)S(1)}, u32[]{:S(2)}, u32[]{:S(2)}) collective-permute-start(f32[8,256]{1,0:T(8,128)S(1)} %get-tuple-element.33), channel_id=1, source_target_pairs={{4,8},{8,4},{12,16},{16,12},{20,24},{24,20},{28,32},{32,28},{36,40... | collective-permute-start | bytes 24584 | tf_op jit(solution)/shard_map/ppermute | solution.py:507
  92.6 3.9 %collective-permute-start.10 = (f32[8,256]{1,0:T(8,128)S(1)}, f32[8,256]{1,0:T(8,128)S(1)}, u32[]{:S(2)}, u32[]{:S(2)}) collective-permute-start(f32[8,256]{1,0:T(8,128)S(1)} %get-tuple-element.35), channel_id=1, source_target_pairs={{0,4},{4,0},{8,12},{12,8},{16,20},{20,16},{24,28},{28,24},{32,36},... | collective-permute-start | bytes 24584 | tf_op jit(solution)/shard_map/ppermute | solution.py:515
  94.5 8.3 %collective-permute-start.11 = (f32[8,256]{1,0:T(8,128)S(1)}, f32[8,256]{1,0:T(8,128)S(1)}, u32[]{:S(2)}, u32[]{:S(2)}) collective-permute-start(f32[8,256]{1,0:T(8,128)S(1)} %get-tuple-element.36), channel_id=1, source_target_pairs={{4,8},{8,4},{12,16},{16,12},{20,24},{24,20},{28,32},{32,28},{36,40... | collective-permute-start | bytes 24584 | tf_op jit(solution)/shard_map/ppermute | solution.py:516
where the time goes:
time: 107 us; the launch traced here: 106 us
  waiting for transfers between devices  36.4 us (34%)
  starting transfers between devices  35 us (33%)
  Pallas kernels  24.2 us (23%)
  local copies, waits for them, and re-layouts  5.79 us (5%)
  other arithmetic  3.26 us (3%)
    ppermute x4, waiting for transfers between devices, per_device(): rb = lax.ppermute(b, 'slab', swap_in)  25.4 us
    pallas_call x3, Pallas kernels, per_device(): call(kernel, 'operator_and_solve_%d' % k, 8, [state, message, message], W...  13.3 us
    pallas_call x1, Pallas kernels, per_device(): call(first_kernel, 'setup_and_solve', 1, [struct(C_ROWS), struct(1536, BF...  8.04 us
    ppermute x4, starting transfers between devices, per_device(): rb = lax.ppermute(b, 'slab', swap_in)  7.7 us
    ppermute x4, starting transfers between devices, per_device(): ra = lax.ppermute(a, 'slab', swap_a)  7.68 us
    all_to_all x1, waiting for transfers between devices, per_device(): lax.all_to_all(jnp.broadcast_to(block[None], (tiles, G_ROWS, PL)), 'tile'...  7.48 us
    ppermute x1, starting transfers between devices, per_device(): lax.ppermute(slots[3], 'slab', [((i + 3) % slabs, i) for i in range(slabs)])  6.8 us
    all_to_all x1, starting transfers between devices, per_device(): lax.all_to_all(jnp.broadcast_to(block[None], (tiles, G_ROWS, PL)), 'tile'...  4.29 us
  transfers between devices with their start and end apart: 13, of which 6 were waited for; matrix products, arithmetic and copies ran while one was open for 5% of the time, Pallas kernels for 0%

commit v1 on v0

v1 whole, which is shorter than its diff:
```python
import jax
import jax.numpy as jnp
from jax import lax
from jax.experimental import pallas as pl
from jax.experimental.pallas import tpu as pltpu
from jax.sharding import PartitionSpec as P


F32 = jnp.float32
BF16 = jnp.bfloat16
NB = 16
PL = 256
CHEB_LOW, CHEB_HIGH = 0.4, 8.0
CENTER = (CHEB_HIGH + CHEB_LOW) / 2.0
HALF = (CHEB_HIGH - CHEB_LOW) / 2.0
SIGMA = CENTER / HALF
RATIO = 1.0 / SIGMA
RATIO_NEXT = 1.0 / (2.0 * SIGMA - RATIO)
STEPS = (
    (0.0, 1.0 / CENTER),
    (RATIO_NEXT * RATIO, 2.0 * RATIO_NEXT / HALF),
) * 2

G_STIFF, G_TABLE, G_EIG, G_ROWS = 64, 76, 88, 96
F_TABLE, F_EIG, F_FACE, F_STIFF, F_ORDER, F_STEP, F_ROWS = 0, 3, 4, 5, 8, 9, 40
C_ACT, C_KX, C_LOAD, C_SLOT, C_ROWS = 0, 256, 384, 640, 656
D_WGT, D_RD, D_FACT, D_GACT, D_FW, D_GW, D_KGG, D_ROWS = 0, 256, 512, 520, 528, 536, 544, 552
S_R, S_U, S_X, S_MF, S_GU, S_ROWS = 0, 256, 512, 768, 776, 784


def iota(shape, dim):
    return lax.broadcasted_iota(jnp.int32, shape, dim)


def split(value):
    high = value.astype(BF16)
    low = (value - high.astype(F32)).astype(BF16)
    return high, low


def dot(a, b):
    return jnp.dot(a, b, preferred_element_type=F32)


def blk(n, base=0, size=NB):
    if isinstance(n, int):
        return slice(base + n * size, base + (n + 1) * size)
    return pl.ds(pl.multiple_of(base + n * size, 8), size)


def loop(count, body, unroll):
    def step(i, carry):
        for k in range(unroll):
            body(i * unroll + k)
        return carry

    lax.fori_loop(0, count // unroll, step, 0)


def apply_weights(value, w_ref, n):
    rows = value.shape[0]
    high, low = split(value)
    both = dot(jnp.concatenate([high, low], axis=0), w_ref[blk(2 * n, 0, PL), :])
    return both[:rows] + both[rows:] + dot(high, w_ref[blk(2 * n + 1, 0, PL), :])


def apply_blocks(bd_ref, which, value, t):
    high, low = split(value)
    m_high = bd_ref[which * 512 + t * 64 : which * 512 + (t + 1) * 64, :64]
    m_low = bd_ref[which * 512 + 256 + t * 64 : which * 512 + 256 + (t + 1) * 64, :64]
    both = dot(jnp.concatenate([m_high, m_low], axis=0), high)
    return both[:64] + both[64:] + dot(m_high, low)


def face_stage(value, mask):
    low, high = value[:, :128], value[:, 128:]
    row = iota((8, 128), 0)
    lane = iota((8, 128), 1)
    before = jnp.where(row % 4 == 0, 0.0, pltpu.roll(high, 1, 0))
    after = jnp.where(row % 4 == 3, 0.0, pltpu.roll(low, 7, 0))
    low = low + jnp.where(lane < 16, pltpu.roll(before, 16, 1), 0.0)
    high = high + jnp.where(lane >= 112, pltpu.roll(after, 112, 1), 0.0)
    return jnp.concatenate([low, high], axis=1) * mask


def assemble(v_ref, ext_ref, xp_ref, c_ref, out):
    row = iota((NB, PL), 0)
    lane = iota((NB, 128), 1)

    def x_stage(t):
        for e in range(4):
            n = t * 4 + e
            m = v_ref[blk(n), :]
            if e > 0:
                left = v_ref[pl.ds(n * NB - 1, 1), :]
            else:
                left = ext_ref[pl.ds(t, 1), :]
            if e < 3:
                right = v_ref[pl.ds(n * NB + NB, 1), :]
            else:
                right = ext_ref[pl.ds(4 + t, 1), :]
            total = m + jnp.where(row == 0, left, 0.0) + jnp.where(row == NB - 1, right, 0.0)
            xp_ref[blk(n + 4), :] = total * c_ref[blk(n, C_ACT), :]

    def y_stage(t):
        for e in range(4):
            n = t * 4 + e
            x = xp_ref[blk(n + 4), :]
            before = xp_ref[blk(n), 128:]
            after = xp_ref[blk(n + 8), :128]
            low = x[:, :128] + jnp.where(lane < 16, pltpu.roll(before, 16, 1), 0.0)
            high = x[:, 128:] + jnp.where(lane >= 112, pltpu.roll(after, 112, 1), 0.0)
            z = jnp.concatenate([low, high], axis=1) * c_ref[blk(n, C_ACT), :]
            out(n, z)

    for t in range(4):
        x_stage(t)
    for t in range(4):
        y_stage(t)


def zero_borders(xp_ref):
    xp_ref[0:64, :] = jnp.zeros((64, PL), F32)
    xp_ref[320:384, :] = jnp.zeros((64, PL), F32)


def phase_one(step, c_ref, d_ref, bd_ref, wf_ref, wb_ref, s_in, s_out, v_ref, v2_ref, xp_ref, ext_ref,
              sm_ref, a_ref, b_ref):
    alpha, beta = step

    def forward(n):
        rows = blk(n)
        value = d_ref[blk(n, D_WGT), :] * s_out[blk(n, S_R), :]
        v2_ref[rows, :] = apply_weights(value, wf_ref, n)

    loop(16, forward, 8)
    for t in range(4):
        h = apply_blocks(bd_ref, 0, v2_ref[t * 64 : t * 64 + 64, :], t)
        h = h * d_ref[D_RD + t * 64 : D_RD + t * 64 + 64, :]
        v2_ref[t * 64 : t * 64 + 64, :] = apply_blocks(bd_ref, 1, h, t)

    def backward(n):
        v_ref[blk(n), :] = c_ref[blk(n, C_ACT), :] * apply_weights(v2_ref[blk(n), :], wb_ref, n)

    loop(16, backward, 8)
    ext_ref[...] = jnp.zeros((8, PL), F32)

    def update(n, z):
        new = beta * (d_ref[blk(n, D_WGT), :] * z)
        if alpha != 0.0:
            new = new + alpha * s_in[blk(n, S_U), :]
        s_out[blk(n, S_U), :] = new

    assemble(v_ref, ext_ref, xp_ref, c_ref, update)
    faces = [v_ref[t * 64 : t * 64 + 1, :] for t in range(4)]
    faces += [v_ref[t * 64 + 63 : t * 64 + 64, :] for t in range(4)]
    faces = jnp.concatenate(faces, axis=0)
    s_out[S_MF : S_MF + 8, :] = faces
    inner = []
    for side in range(2):
        for t in range(4):
            n = t * 4 + 3 * side
            k = c_ref[blk(side * 4 + t, C_KX), :]
            inner.append(jnp.sum(k * s_out[blk(n, S_U), :], axis=0, keepdims=True))
    inner = jnp.concatenate(inner, axis=0)
    to_left = jnp.concatenate([faces[:4], inner[:4]], axis=0)
    to_right = jnp.concatenate([faces[4:], inner[4:]], axis=0)
    even = jnp.full((8, PL), sm_ref[0], jnp.int32) == 0
    a_ref[...] = jnp.where(even, to_right, to_left)
    b_ref[...] = jnp.where(even, to_left, to_right)


def phase_two(step, c_ref, d_ref, bk_ref, m_ref, mg_ref, s_in, s_out, v_ref, v2_ref, xp_ref, ext_ref, sm_ref,
              a_ref, b_ref):
    alpha, beta = step
    even = jnp.full((8, PL), sm_ref[0], jnp.int32) == 0
    rec_a, rec_b = a_ref[...], b_ref[...]
    from_left = jnp.where(even, rec_b, rec_a)
    from_right = jnp.where(even, rec_a, rec_b)
    outer = jnp.concatenate([from_left[:4], from_right[:4]], axis=0)
    inner = jnp.concatenate([from_left[4:], from_right[4:]], axis=0)
    fact = d_ref[D_FACT : D_FACT + 8, :]
    gact = d_ref[D_GACT : D_GACT + 8, :]
    delta = beta * (d_ref[D_FW : D_FW + 8, :] * face_stage(fact * outer, fact))
    ghost = (outer + s_in[S_MF : S_MF + 8, :]) * gact
    ghost = beta * (d_ref[D_GW : D_GW + 8, :] * face_stage(ghost, gact))
    if alpha != 0.0:
        ghost = ghost + alpha * s_in[S_GU : S_GU + 8, :]
    s_out[S_GU : S_GU + 8, :] = ghost
    row = iota((NB, PL), 0)
    for t in range(4):
        for e in range(4):
            n = t * 4 + e
            u = s_in[blk(n, S_U), :]
            if e == 0:
                u = u + jnp.where(row == 0, delta[t : t + 1], 0.0)
            if e == 3:
                u = u + jnp.where(row == NB - 1, delta[4 + t : 5 + t], 0.0)
            s_out[blk(n, S_U), :] = u
            s_out[blk(n, S_X), :] = s_in[blk(n, S_X), :] + u

    for t in range(4):
        v2_ref[t * 64 : t * 64 + 64, :] = apply_blocks(
            bk_ref, 0, s_out[S_U + t * 64 : S_U + t * 64 + 64, :], t
        )
    high, low = split(ghost)
    both = jnp.concatenate([high, low], axis=0)
    row8 = iota((8, PL), 0)
    image = inner + d_ref[D_KGG : D_KGG + 8, :] * ghost
    for s in range(8):
        w = s
        part = dot(both, mg_ref[blk(2 * w, 0, PL), :])
        part = part[:8] + part[8:] + dot(high, mg_ref[blk(2 * w + 1, 0, PL), :])
        image = image + jnp.where(row8 == s, part, 0.0)
    ext_ref[...] = image * gact

    def local(n):
        rows = blk(n)
        q = v2_ref[rows, :] + apply_weights(s_out[blk(n, S_U), :], m_ref, n)
        v_ref[rows, :] = c_ref[blk(n, C_ACT), :] * q

    loop(16, local, 8)

    def update(n, z):
        s_out[blk(n, S_R), :] = s_in[blk(n, S_R), :] - z

    assemble(v_ref, ext_ref, xp_ref, c_ref, update)


OWN = [(t, e) for t in range(4) for e in range(4)]


def hot(condition):
    return jnp.where(condition, 1.0, 0.0).astype(BF16)


def hots():
    l, m = iota((PL, PL), 0), iota((PL, PL), 1)
    return (l, m, hot(l % NB == m // NB), hot(l % NB == m % NB), hot(l // NB == m // NB),
            hot(l // NB == m % NB))


def expand(p_ref, rows, mask, onehot):
    for i, row in enumerate(rows):
        p_ref[blk(i), :] = jnp.where(mask, row, 0.0)
    for start in range(0, len(rows) * NB, 128):
        high, low = split(p_ref[start : start + 128, :])
        yield start, dot(high, onehot) + dot(low, onehot)


def block_rows(bd_ref, which, parts):
    block = (iota((128, PL), 0) // NB) % 4 == iota((128, PL), 1) // NB
    for start, part in parts:
        high, low = split(jnp.where(block, part, 0.0))
        bd_ref[which * 512 + start : which * 512 + start + 128, :] = high
        bd_ref[which * 512 + 256 + start : which * 512 + 256 + start + 128, :] = low


def store_pair(w_ref, n, j, value):
    high, low = split(value)
    w_ref[pl.ds(pl.multiple_of(n * 512 + j * NB, 16), NB), :] = high
    w_ref[pl.ds(pl.multiple_of(n * 512 + 256 + j * NB, 16), NB), :] = low


def build_sums(m_ref, count, ta_ref, tb_ref):
    lane = iota((NB, PL), 1)
    by_col = lane % NB == iota((NB, PL), 0)

    def build(n):
        ty = ta_ref[blk(n), :]
        tz = tb_ref[blk(n), :]
        for j in range(NB):
            value = jnp.where(by_col, ty[j : j + 1, :], 0.0)
            store_pair(m_ref, n, j, value + jnp.where(lane // NB == j, tz, 0.0))

    loop(count, build, 2)


def along(index, order):
    return jnp.where((index.astype(F32) < order) | (index == NB - 1), 1.0, 0.0)


def side_stack(pick):
    return jnp.concatenate([pick(0, t) for t in range(4)] + [pick(1, t) for t in range(4)], axis=0)


def edge_rows(ref, base):
    return side_stack(
        lambda side, t: ref[base + t * 64 + 63 * side : base + t * 64 + 63 * side + 1, :]
    )


def pack_kernel(ord_hbm, route_hbm, load_hbm, stiff_hbm, table_hbm, eig_hbm, o_ref,
                ord_ref, route_ref, load_ref, stiff_ref, table_ref, eig_ref, sems):
    copies = [
        pltpu.make_async_copy(src, dst, sems.at[i])
        for i, (src, dst) in enumerate(
            ((load_hbm, load_ref), (stiff_hbm, stiff_ref), (table_hbm, table_ref),
             (eig_hbm, eig_ref), (ord_hbm, ord_ref), (route_hbm, route_ref))
        )
    ]
    for copy in copies:
        copy.start()
    lane = iota((1, PL), 1)
    for d in range(4):
        o_ref[d, 92:96, :] = jnp.zeros((4, PL), F32)
    for copy in copies:
        copy.wait()
    for d in range(4):
        o_ref[d, 0:64, :] = load_ref[...]
    for e in range(4):
        order = jnp.full((1, PL), ord_ref[e], jnp.int32).astype(F32)
        slot = jnp.full((1, PL), lax.rem(route_ref[e], 4), jnp.int32).astype(F32)
        tail = jnp.where(lane == 48, order, jnp.where(lane == 49, slot, 0.0))
        for d in range(4):
            for k in range(3):
                r = 3 * e + k
                o_ref[d, G_STIFF + r : G_STIFF + r + 1, :] = stiff_ref[e : e + 1, k * PL : (k + 1) * PL]
                o_ref[d, G_TABLE + r : G_TABLE + r + 1, :] = table_ref[e : e + 1, k * PL : (k + 1) * PL]
            o_ref[d, G_EIG + e : G_EIG + e + 1, :] = tail
            o_ref[d, G_EIG + e : G_EIG + e + 1, 0:48] = eig_ref[e : e + 1, :]


def pick_kernel(sm_ref, g_ref, a_ref, b_ref, t2_ref, t3_ref, l_ref, r_ref):
    for t in range(4):
        base = t * F_STEP
        for ref, e in ((l_ref, 0), (r_ref, 3)):
            face = e * NB + (NB - 1 if e else 0)
            slot = 1 if e == 0 else 0
            ref[base + F_TABLE : base + F_TABLE + 3, :] = g_ref[t, G_TABLE + 3 * slot : G_TABLE + 3 * slot + 3, :]
            ref[base + F_EIG : base + F_EIG + 1, :] = g_ref[t, G_EIG + slot : G_EIG + slot + 1, :]
            ref[base + F_FACE : base + F_FACE + 1, :] = g_ref[t, face : face + 1, :]
            ref[base + F_STIFF : base + F_STIFF + 3, :] = g_ref[t, G_STIFF + 3 * e : G_STIFF + 3 * e + 3, :]
            ref[base + F_ORDER : base + F_ORDER + 1, :] = g_ref[t, G_EIG + e : G_EIG + e + 1, :]
        for ref, slot in ((t2_ref, 2), (t3_ref, 3)):
            ref[4 * t : 4 * t + 3, :] = g_ref[t, G_TABLE + 3 * slot : G_TABLE + 3 * slot + 3, :]
            ref[4 * t + 3 : 4 * t + 4, :] = g_ref[t, G_EIG + slot : G_EIG + slot + 1, :]
    l_ref[36:40, :] = jnp.zeros((4, PL), F32)
    r_ref[36:40, :] = jnp.zeros((4, PL), F32)
    even = jnp.full((F_ROWS, PL), sm_ref[0], jnp.int32) == 0
    to_left, to_right = l_ref[...], r_ref[...]
    a_ref[...] = jnp.where(even, to_right, to_left)
    b_ref[...] = jnp.where(even, to_left, to_right)


def slab_kernel(sm_ref, g_ref, c_ref, bk_ref, m_ref, p_ref, ta_ref, tb_ref):
    row = iota((NB, PL), 0)
    lane = iota((NB, PL), 1)
    l, _, _, e2, e3, e4 = hots()

    def stiff(d):
        return [g_ref[t, G_STIFF + 3 * e + d : G_STIFF + 3 * e + d + 1, :] for t, e in OWN]

    block_rows(bk_ref, 0, expand(p_ref, stiff(0), lane // NB == row, e2))
    eig = jnp.concatenate([g_ref[t, G_EIG : G_EIG + 4, :] for t in range(4)], axis=0)
    ints = eig.astype(BF16)
    orders = dot(ints, hot(l == 48))
    c_ref[C_SLOT : C_SLOT + 16, :] = dot(ints, hot(l == 49))
    for n, (t, e) in enumerate(OWN):
        order = orders[n : n + 1, :]
        act = along(row, order) * (along(lane // NB, order) * along(lane % NB, order))
        c_ref[blk(n, C_ACT), :] = act
        c_ref[blk(n, C_LOAD), :] = act * g_ref[t, e * NB : (e + 1) * NB, :]
    for side in range(2):
        for t in range(4):
            e = 3 * side
            kx = g_ref[t, G_STIFF + 3 * e : G_STIFF + 3 * e + 1, :]
            edge = NB - 1 if side else 0
            col = jnp.sum(
                jnp.where((lane == edge * NB + row) & (row != edge), kx, 0.0), axis=1, keepdims=True
            )
            c_ref[blk(side * 4 + t, C_KX), :] = jnp.broadcast_to(col, (NB, PL))
    for start, part in expand(p_ref, stiff(1), lane % NB == row, e3):
        ta_ref[start : start + 128, :] = part
    for start, part in expand(p_ref, stiff(2), lane % NB == row, e4):
        tb_ref[start : start + 128, :] = part
    build_sums(m_ref, 16, ta_ref, tb_ref)


def first_kernel(sm_ref, g_ref, ra_ref, rb_ref, t2_ref, t3_ref, c_ref, m_ref, d_ref, bd_ref, wf_ref, wb_ref, mg_ref, s_ref, a_ref,
                 b_ref, v_ref, v2_ref, xp_ref, ext_ref, p_ref, ta_ref, tb_ref, h_ref, f_ref):
    even = jnp.full((F_ROWS, PL), sm_ref[0], jnp.int32) == 0
    rec_a, rec_b = ra_ref[...], rb_ref[...]
    f_ref[0] = jnp.where(even, rec_b, rec_a)
    f_ref[1] = jnp.where(even, rec_a, rec_b)
    zero_borders(xp_ref)
    row = iota((NB, PL), 0)
    lane = iota((NB, PL), 1)
    by_row = lane // NB == row
    by_col = lane % NB == row
    l, m, e1, e2, e3, e4 = hots()
    lane8 = iota((8, PL), 1)
    row8 = iota((8, PL), 0)

    for n, (t, e) in enumerate(OWN):
        slot = c_ref[C_SLOT + n : C_SLOT + n + 1, :]
        found = jnp.where(
            slot == 0.0,
            jnp.concatenate([g_ref[t, G_TABLE : G_TABLE + 3, :], g_ref[t, G_EIG : G_EIG + 1, :]], axis=0),
            0.0,
        )
        others = (
            f_ref[1, t * F_STEP : t * F_STEP + 4, :],
            t2_ref[4 * t : 4 * t + 4, :],
            t3_ref[4 * t : 4 * t + 4, :],
        )
        for g in range(3):
            found = jnp.where(slot == float(g + 1), others[g], found)
        h_ref[n * 8 : n * 8 + 4, :] = found

    def basis(d):
        return [h_ref[n * 8 + d : n * 8 + d + 1, :] for n in range(16)]

    block_rows(bd_ref, 0, expand(p_ref, basis(0), by_col, e4))
    block_rows(bd_ref, 1, expand(p_ref, basis(0), by_row, e2))
    eig = jnp.concatenate(basis(3), axis=0)
    high, low = split(eig)
    cross_hot = hot(l == 16 + m // NB) + hot(l == 32 + m % NB)
    cross = dot(high, cross_hot) + dot(low, cross_hot)
    for start, part in expand(p_ref, basis(3), lane == row, hot(l < 16)):
        v_ref[start : start + 128, :] = part
    for n in range(16):
        d_ref[blk(n, D_RD), :] = 1.0 / (v_ref[blk(n), :] + cross[n : n + 1, :])

    def ghost(r):
        return side_stack(
            lambda side, t: f_ref[side, t * F_STEP + r : t * F_STEP + r + 1, :]
        )

    there = jnp.where(row8 < 4, sm_ref[2], sm_ref[3]) > 0
    order = dot(ghost(F_ORDER).astype(BF16), hot(l == 48))
    gact = jnp.where(there, along(lane8 // NB, order) * along(lane8 % NB, order), 0.0)
    fact = edge_rows(c_ref, C_ACT)
    d_ref[D_FACT : D_FACT + 8, :] = fact
    d_ref[D_GACT : D_GACT + 8, :] = gact
    ghost_shares = face_stage((gact + fact) * gact, gact)
    d_ref[D_GW : D_GW + 8, :] = gact / jnp.maximum(ghost_shares, 1.0)
    pick = lane8 == jnp.where(row8 < 4, PL - 1, 0)
    kgg = jnp.sum(jnp.where(pick, ghost(F_STIFF), 0.0), axis=1, keepdims=True)
    d_ref[D_KGG : D_KGG + 8, :] = jnp.broadcast_to(kgg, (8, PL))

    v_ref[...] = c_ref[C_ACT : C_ACT + 256, :]
    ext_ref[...] = gact

    def weigh(n, z):
        d_ref[blk(n, D_WGT), :] = c_ref[blk(n, C_ACT), :] / jnp.maximum(z, 1.0)

    assemble(v_ref, ext_ref, xp_ref, c_ref, weigh)
    d_ref[D_FW : D_FW + 8, :] = edge_rows(d_ref, D_WGT)
    v_ref[...] = c_ref[C_LOAD : C_LOAD + 256, :]
    ext_ref[...] = gact * ghost(F_FACE)

    def start_residual(n, z):
        s_ref[blk(n, S_R), :] = z

    assemble(v_ref, ext_ref, xp_ref, c_ref, start_residual)
    s_ref[S_X : S_X + 256, :] = jnp.zeros((256, PL), F32)
    s_ref[S_GU : S_GU + 8, :] = jnp.zeros((8, PL), F32)

    def product(w_ref, mask, hot_y, hot_z):
        for start, part in expand(p_ref, basis(1), mask, hot_y):
            ta_ref[start : start + 128, :] = part
        for start, part in expand(p_ref, basis(2), mask, hot_z):
            tb_ref[start : start + 128, :] = part

        def build(n):
            ty = ta_ref[blk(n), :]
            tz = tb_ref[blk(n), :]
            for b in range(NB):
                store_pair(w_ref, n, b, ty[b : b + 1, :] * tz)

        loop(16, build, 2)

    product(wf_ref, by_row, e1, e2)
    product(wb_ref, by_col, e3, e4)

    def ghost_list(r):
        return [f_ref[side, t * F_STEP + r : t * F_STEP + r + 1, :]
                for side in range(2) for t in range(4)]

    for start, part in expand(p_ref, ghost_list(F_STIFF + 1), by_col, e3):
        ta_ref[start : start + 128, :] = part
    for start, part in expand(p_ref, ghost_list(F_STIFF + 2), by_col, e4):
        tb_ref[start : start + 128, :] = part
    build_sums(mg_ref, 8, ta_ref, tb_ref)
    phase_one(STEPS[0], c_ref, d_ref, bd_ref, wf_ref, wb_ref, s_ref, s_ref, v_ref, v2_ref, xp_ref,
              ext_ref, sm_ref, a_ref, b_ref)


def middle_kernel(k, sm_ref, ra_ref, rb_ref, c_ref, d_ref, bd_ref, bk_ref, wf_ref, wb_ref, m_ref,
                  mg_ref, si_ref, so_ref, a_ref, b_ref, v_ref, v2_ref, xp_ref, ext_ref):
    zero_borders(xp_ref)
    phase_two(STEPS[k], c_ref, d_ref, bk_ref, m_ref, mg_ref, si_ref, so_ref, v_ref, v2_ref, xp_ref,
              ext_ref, sm_ref, ra_ref, rb_ref)
    phase_one(STEPS[k + 1], c_ref, d_ref, bd_ref, wf_ref, wb_ref, so_ref, so_ref, v_ref, v2_ref,
              xp_ref, ext_ref, sm_ref, a_ref, b_ref)


def last_kernel(sm_ref, ra_ref, rb_ref, c_ref, d_ref, bk_ref, m_ref, mg_ref, si_ref, x_ref, r_ref,
                so_ref, v_ref, v2_ref, xp_ref, ext_ref):
    zero_borders(xp_ref)
    phase_two(STEPS[3], c_ref, d_ref, bk_ref, m_ref, mg_ref, si_ref, so_ref, v_ref, v2_ref, xp_ref,
              ext_ref, sm_ref, ra_ref, rb_ref)
    base = pl.multiple_of(sm_ref[1] * 64, 64)
    x_ref[...] = so_ref[pl.ds(S_X + base, 64), :]
    r_ref[...] = so_ref[pl.ds(S_R + base, 64), :]


VM = pl.BlockSpec(memory_space=pltpu.VMEM)
SM = pl.BlockSpec(memory_space=pltpu.SMEM)


def struct(rows, dtype=F32):
    return jax.ShapeDtypeStruct((rows, PL), dtype)


WORK = [pltpu.VMEM((256, PL), F32), pltpu.VMEM((256, PL), F32), pltpu.VMEM((384, PL), F32),
        pltpu.VMEM((8, PL), F32)]
LIMIT = pltpu.CompilerParams(vmem_limit_bytes=12 * 2**20)


def call(kernel, scalars, ins, outs, scratch=(), flops=2 * 10**9, where=VM):
    return pl.pallas_call(
        kernel,
        in_specs=[SM] * scalars + [where] * ins,
        out_specs=[VM] * len(outs),
        out_shape=outs,
        scratch_shapes=list(scratch),
        compiler_params=LIMIT,
        cost_estimate=pl.CostEstimate(flops=flops, transcendentals=0, bytes_accessed=2**20),
    )


def per_device(load_field, orders, stiffness, basis_table, eigen_values, route_plan):
    slabs = lax.axis_size("slab")
    tiles = lax.axis_size("tile")
    p = lax.axis_index("slab")
    tile = lax.axis_index("tile")
    scalars = jnp.stack([p % 2, tile, p, slabs - 1 - p]).astype(jnp.int32)
    swap_a = [(i, i ^ 1) for i in range(slabs)]
    swap_b = [(i, i + 1 if i % 2 else i - 1) for i in range(1, slabs - 1)]
    ring_b = [(i, (i + 1 if i % 2 else i - 1) % slabs) for i in range(slabs)]

    def gather(block):
        return lax.all_to_all(block, "tile", 0, 0)

    def ahead(block, distance):
        return lax.ppermute(block, "slab", [((i + distance) % slabs, i) for i in range(slabs)])

    (packed,) = call(
        pack_kernel, 0, 6, [jax.ShapeDtypeStruct((tiles, G_ROWS, PL), F32)],
        [pltpu.SMEM((4,), jnp.int32), pltpu.SMEM((4,), jnp.int32), pltpu.VMEM((64, PL), F32),
         pltpu.VMEM((4, 768), F32), pltpu.VMEM((4, 768), F32), pltpu.VMEM((4, 48), F32),
         pltpu.SemaphoreType.DMA((6,))],
        where=pl.BlockSpec(memory_space=pltpu.HBM),
    )(*[pltpu.with_memory_space_constraint(item, pltpu.HBM) for item in (
        orders, route_plan, load_field.reshape(64, PL), stiffness, basis_table, eigen_values)])
    slab = gather(packed)
    pa, pb, p2, p3 = call(
        pick_kernel, 1, 1, [struct(F_ROWS), struct(F_ROWS), struct(16), struct(16)],
        [pltpu.VMEM((F_ROWS, PL), F32)] * 2,
    )(scalars, slab)
    wide = pltpu.VMEM((256, PL), F32)
    rb = lax.ppermute(pb, "slab", ring_b)
    t3 = ahead(p3, 3)
    t2 = ahead(p2, 2)
    ra = lax.ppermute(pa, "slab", swap_a)
    consts, blocks_k, w_m = call(
        slab_kernel, 1, 1, [struct(C_ROWS), struct(512, BF16), struct(16 * 512, BF16)],
        [wide] * 3,
    )(scalars, slab)

    def exchange(a, b):
        rb = lax.ppermute(b, "slab", swap_b)
        ra = lax.ppermute(a, "slab", swap_a)
        return ra, rb

    message = struct(8)
    more, blocks, w_f, w_b, w_g, s, a, b = call(
        first_kernel,
        1,
        7,
        [struct(D_ROWS), struct(1024, BF16), struct(16 * 512, BF16), struct(16 * 512, BF16),
         struct(8 * 512, BF16), struct(S_ROWS), message, message],
        WORK + [wide] * 3 + [pltpu.VMEM((128, PL), F32), pltpu.VMEM((2, F_ROWS, PL), F32)],
    )(scalars, slab, ra, rb, t2, t3, consts, w_m)
    for k in range(3):
        ra, rb = exchange(a, b)

        def kernel(*refs, k=k):
            middle_kernel(k, *refs)

        s, a, b = call(
            kernel, 1, 11, [struct(S_ROWS), message, message], WORK
        )(scalars, ra, rb, consts, more, blocks, blocks_k, w_f, w_b, w_m, w_g, s)
    ra, rb = exchange(a, b)
    x, r = call(
        last_kernel, 1, 8, [struct(64), struct(64)],
        [pltpu.VMEM((S_ROWS, PL), F32)] + WORK,
    )(scalars, ra, rb, consts, more, blocks_k, w_m, w_g, s)
    return x.reshape(load_field.shape), r.reshape(load_field.shape)


def solution(mesh):
    both = ("slab", "tile")
    in_specs = (P(both, None, None), P(both), P(both, None), P(both, None), P(both, None), P(both))
    out_specs = (P(both, None, None), P(both, None, None))
    return jax.shard_map(
        per_device, mesh=mesh, in_specs=in_specs, out_specs=out_specs, check_vma=False
    )
```

time: 107 us -> 100 us (0.935)
  local copies, waits for them, and re-layouts: 5.79 us -> 0 us
  starting transfers between devices: 35 us -> 38.2 us
  waiting for transfers between devices: 36.4 us -> 33.2 us
  other arithmetic: 3.26 us -> 0.08 us
  Pallas kernels: 24.2 us -> 27.3 us
    ppermute x12, waiting for transfers between devices: 28.9 us -> 25.2 us  [the longest x4 21.6 us: exchange(): rb = lax.ppermute(b, 'slab', swap_b)]
    pallas_call x5 -> x8, Pallas kernels: 24.2 us -> 27.3 us  [the longest x3 13.3 us: per_device(): call(kernel, 1, 11, [struct(S_ROWS), message, message], WORK)]
    ppermute x12, starting transfers between devices: 30.7 us -> 33.9 us  [the longest x4 11.4 us: exchange(): rb = lax.ppermute(b, 'slab', swap_b)]
    slice x7 -> x0, local copies, waits for them, and re-layouts: 1.55 us -> none  [the longest x1 0.8 us: per_device(): stiff[0]]
    broadcast_in_dim x4 -> x0, local copies, waits for them, and re-layouts: 1.48 us -> none  [the longest x1 0.79 us: per_device(): jnp.broadcast_to(block[None], (tiles, G_ROWS, PL))]
    concatenate x2 -> x0, local copies, waits for them, and re-layouts: 1.28 us -> none  [the longest x1 1.2 us: per_device(): jnp.concatenate([load_field.reshape(64, PL), stiff.reshape(12, PL), from_...]
  transfers between devices with their start and end apart: 13 -> 13, of which waited for: 6 -> 6; matrix products, arithmetic and copies ran while one was open for 5% -> 0% of each run, Pallas kernels for 0% -> 2%
where the time goes in v1:
time: 100 us; the launch traced here: 99.6 us
  starting transfers between devices  38.2 us (38%)
  waiting for transfers between devices  33.2 us (33%)
  Pallas kernels  27.3 us (27%)
    ppermute x4, waiting for transfers between devices, exchange(): rb = lax.ppermute(b, 'slab', swap_b)  21.6 us
    pallas_call x3, Pallas kernels, per_device(): call(kernel, 1, 11, [struct(S_ROWS), message, message], WORK)  13.3 us
    ppermute x4, starting transfers between devices, exchange(): rb = lax.ppermute(b, 'slab', swap_b)  11.4 us
    ppermute x2, starting transfers between devices, ahead(): lax.ppermute(block, 'slab', [((i + distance) % slabs, i) for i in range(s...  8.5 us
    all_to_all x1, waiting for transfers between devices, gather(): return lax.all_to_all(block, 'tile', 0, 0)  8 us
    ppermute x4, starting transfers between devices, exchange(): ra = lax.ppermute(a, 'slab', swap_a)  7.68 us
    pallas_call x1, Pallas kernels, per_device(): call(first_kernel, 1, 7, [struct(D_ROWS), struct(1024, BF16), struct(16 *...  6.73 us
    all_to_all x1, starting transfers between devices, gather(): return lax.all_to_all(block, 'tile', 0, 0)  4.3 us
  transfers between devices with their start and end apart: 13, of which 6 were waited for; matrix products, arithmetic and copies ran while one was open for 0% of the time, Pallas kernels for 2%

profile of v1, /device:TPU:512, one launch (start us, length us, event | category | flops | bytes accessed | tf_op | source)
XLA Modules:
  0.0 99.6 jit_solution(6504800364745137437)
XLA Ops:
  0.6 1.7 %shard_map.77 = f32[4,96,256]{2,1,0:T(8,128)} custom-call(s32[4]{0:T(128)} %ord_hbm.1, s32[4]{0:T(128)} %route_hbm.1, f32[64,256]{1,0:T(8,128)} %bitcast.7, f32[4,768]{1,0:T(4,128)} %stiff_hbm.1, f32[4,768]{1,0:T(4,128)} %table_hbm.1, f32[4,48]{1,0:T(4,128)} %eig_hbm.1), custom_call_target="tpu_custom_call" | custom-call | flops 2000000000 | bytes 1048576 | tf_op jit(solution)/shard_map/pallas_call | solution.py:550
  2.4 4.3 %all-to-all-start = ((f32[4,96,256]{2,1,0:T(8,128)}), f32[4,96,256]{2,1,0:T(8,128)S(1)}, u32[]{:S(2)}, u32[]{:S(2)}) async-start(f32[4,96,256]{2,1,0:T(8,128)} %shard_map.77), calls=%async_computation | async-start | bytes 786432 | tf_op jit(solution)/shard_map/all_to_all | solution.py:545
  6.7 0.1 pad_add_fusion.sm_ref.refs_0_
  6.7 8.0 %all-to-all-done.g_ref = f32[4,96,256]{2,1,0:T(8,128)S(1)} async-done(((f32[4,96,256]{2,1,0:T(8,128)}), f32[4,96,256]{2,1,0:T(8,128)S(1)}, u32[]{:S(2)}, u32[]{:S(2)}) %all-to-all-start) | async-done | bytes 393248 | tf_op jit(solution)/shard_map/all_to_all | solution.py:545
  14.7 0.6 shard_map.78
  15.3 6.6 %collective-permute-start.2 = (f32[16,256]{1,0:T(8,128)S(1)}, f32[16,256]{1,0:T(8,128)S(1)}, u32[]{:S(2)}, u32[]{:S(2)}) collective-permute-start(f32[16,256]{1,0:T(8,128)S(1)} %get-tuple-element.30), channel_id=1, source_target_pairs={{8,0},{12,4},{16,8},{20,12},{24,16},{28,20},{32,24},{36,28},{40,32... | collective-permute-start | bytes 49160 | tf_op jit(solution)/shard_map/ppermute | solution.py:548
  21.9 1.9 %collective-permute-start.3 = (f32[16,256]{1,0:T(8,128)S(1)}, f32[16,256]{1,0:T(8,128)S(1)}, u32[]{:S(2)}, u32[]{:S(2)}) collective-permute-start(f32[16,256]{1,0:T(8,128)S(1)} %get-tuple-element.31), channel_id=1, source_target_pairs={{12,0},{16,4},{20,8},{24,12},{28,16},{32,20},{36,24},{40,28},{44,3... | collective-permute-start | bytes 49160 | tf_op jit(solution)/shard_map/ppermute | solution.py:548
  23.8 3.4 %collective-permute-start = (f32[40,256]{1,0:T(8,128)S(1)}, f32[40,256]{1,0:T(8,128)S(1)}, u32[]{:S(2)}, u32[]{:S(2)}) collective-permute-start(f32[40,256]{1,0:T(8,128)S(1)} %get-tuple-element.28), channel_id=1, source_target_pairs={{0,4},{4,0},{8,12},{12,8},{16,20},{20,16},{24,28},{28,24},{32,36},... | collective-permute-start | bytes 122888 | tf_op jit(solution)/shard_map/ppermute | solution.py:567
  27.2 2.9 %collective-permute-start.1 = (f32[40,256]{1,0:T(8,128)S(1)}, f32[40,256]{1,0:T(8,128)S(1)}, u32[]{:S(2)}, u32[]{:S(2)}) collective-permute-start(f32[40,256]{1,0:T(8,128)S(1)} %get-tuple-element.29), channel_id=1, source_target_pairs={{0,764},{4,8},{8,4},{12,16},{16,12},{20,24},{24,20},{28,32},{32,28... | collective-permute-start | bytes 122888 | tf_op jit(solution)/shard_map/ppermute | solution.py:564
  30.1 2.2 %shard_map.79 = (f32[656,256]{1,0:T(8,128)S(1)}, bf16[512,256]{1,0:T(8,128)(2,1)S(1)}, bf16[8192,256]{1,0:T(8,128)(2,1)S(1)}) custom-call(s32[4]{0:T(128)S(1)} %pad_add_fusion.sm_ref.refs_0_, f32[4,96,256]{2,1,0:T(8,128)S(1)} %all-to-all-done.g_ref), custom_call_target="tpu_custom_call" | custom-call | flops 2000000000 | bytes 1048576 | tf_op jit(solution)/shard_map/pallas_call | solution.py:568
  32.3 0.0 collective-permute-done.2.t2_ref
  32.3 0.0 collective-permute-done.3.t3_ref
  32.3 0.0 collective-permute-done.ra_ref
  32.3 3.5 %collective-permute-done.1.rb_ref = f32[40,256]{1,0:T(8,128)S(1)} collective-permute-done((f32[40,256]{1,0:T(8,128)S(1)}, f32[40,256]{1,0:T(8,128)S(1)}, u32[]{:S(2)}, u32[]{:S(2)}) %collective-permute-start.1) | collective-permute-done | bytes 40992 | tf_op jit(solution)/shard_map/ppermute | solution.py:564
  35.9 6.7 %shard_map.80 = (f32[552,256]{1,0:T(8,128)S(1)}, bf16[1024,256]{1,0:T(8,128)(2,1)S(1)}, bf16[8192,256]{1,0:T(8,128)(2,1)S(1)}, bf16[8192,256]{1,0:T(8,128)(2,1)S...) custom-call(s32[4]{0:T(128)S(1)} %pad_add_fusion.sm_ref.refs_0_, ...), custom_call_target="tpu_custom_call" | custom-call | flops 2000000000 | bytes 1048576 | tf_op jit(solution)/shard_map/pallas_call | solution.py:579
  42.6 1.9 %collective-permute-start.4 = (f32[8,256]{1,0:T(8,128)S(1)}, f32[8,256]{1,0:T(8,128)S(1)}, u32[]{:S(2)}, u32[]{:S(2)}) collective-permute-start(f32[8,256]{1,0:T(8,128)S(1)} %get-tuple-element.34), channel_id=1, source_target_pairs={{0,4},{4,0},{8,12},{12,8},{16,20},{20,16},{24,28},{28,24},{32,36},... | collective-permute-start | bytes 24584 | tf_op jit(solution)/shard_map/ppermute | solution.py:575
  44.5 2.9 %collective-permute-start.5 = (f32[8,256]{1,0:T(8,128)S(1)}, f32[8,256]{1,0:T(8,128)S(1)}, u32[]{:S(2)}, u32[]{:S(2)}) collective-permute-start(f32[8,256]{1,0:T(8,128)S(1)} %get-tuple-element.35), channel_id=1, source_target_pairs={{4,8},{8,4},{12,16},{16,12},{20,24},{24,20},{28,32},{32,28},{36,40... | collective-permute-start | bytes 24584 | tf_op jit(solution)/shard_map/ppermute | solution.py:574
  47.4 0.0 collective-permute-done.4.refs_1_
  47.4 5.4 %collective-permute-done.5.refs_2_ = f32[8,256]{1,0:T(8,128)S(1)} collective-permute-done((f32[8,256]{1,0:T(8,128)S(1)}, f32[8,256]{1,0:T(8,128)S(1)}, u32[]{:S(2)}, u32[]{:S(2)}) %collective-permute-start.5) | collective-permute-done | bytes 8224 | tf_op jit(solution)/shard_map/ppermute | solution.py:574
  52.8 4.4 %shard_map.81 = (f32[784,256]{1,0:T(8,128)S(1)}, f32[8,256]{1,0:T(8,128)S(1)}, f32[8,256]{1,0:T(8,128)S(1)}) custom-call(s32[4]{0:T(128)S(1)} %pad_add_fusion.sm_ref.refs_0_, f32[8,256]{1,0:T(8,128)S(1)} %collective-permute-done.4.refs_1_, f32[8,256]{1,0:T(8,128)S(1)} %collective-permute-done.5.refs_2_, f32[656,256]{1,0:T(8,128)S(1)} %get-tuple-element.32.c_ref.refs_3_, ...), custom_call_target="tpu_custom_call" | custom-call | flops 2000000000 | bytes 1048576 | tf_op jit(solution)/shard_map/pallas_call | solution.py:593
  57.3 1.9 %collective-permute-start.6 = (f32[8,256]{1,0:T(8,128)S(1)}, f32[8,256]{1,0:T(8,128)S(1)}, u32[]{:S(2)}, u32[]{:S(2)}) collective-permute-start(f32[8,256]{1,0:T(8,128)S(1)} %get-tuple-element.43), channel_id=1, source_target_pairs={{0,4},{4,0},{8,12},{12,8},{16,20},{20,16},{24,28},{28,24},{32,36},... | collective-permute-start | bytes 24584 | tf_op jit(solution)/shard_map/ppermute | solution.py:575
  59.2 2.9 %collective-permute-start.7 = (f32[8,256]{1,0:T(8,128)S(1)}, f32[8,256]{1,0:T(8,128)S(1)}, u32[]{:S(2)}, u32[]{:S(2)}) collective-permute-start(f32[8,256]{1,0:T(8,128)S(1)} %get-tuple-element.44), channel_id=1, source_target_pairs={{4,8},{8,4},{12,16},{16,12},{20,24},{24,20},{28,32},{32,28},{36,40... | collective-permute-start | bytes 24584 | tf_op jit(solution)/shard_map/ppermute | solution.py:574
  62.1 0.0 collective-permute-done.6.refs_1_
  62.1 5.4 %collective-permute-done.7.refs_2_ = f32[8,256]{1,0:T(8,128)S(1)} collective-permute-done((f32[8,256]{1,0:T(8,128)S(1)}, f32[8,256]{1,0:T(8,128)S(1)}, u32[]{:S(2)}, u32[]{:S(2)}) %collective-permute-start.7) | collective-permute-done | bytes 8224 | tf_op jit(solution)/shard_map/ppermute | solution.py:574
  67.5 4.4 %shard_map.82 = (f32[784,256]{1,0:T(8,128)S(1)}, f32[8,256]{1,0:T(8,128)S(1)}, f32[8,256]{1,0:T(8,128)S(1)}) custom-call(s32[4]{0:T(128)S(1)} %pad_add_fusion.sm_ref.refs_0_, f32[8,256]{1,0:T(8,128)S(1)} %collective-permute-done.6.refs_1_, f32[8,256]{1,0:T(8,128)S(1)} %collective-permute-done.7.refs_2_, f32[656,256]{1,0:T(8,128)S(1)} %get-tuple-element.32.c_ref.refs_3_, ...), custom_call_target="tpu_custom_call" | custom-call | flops 2000000000 | bytes 1048576 | tf_op jit(solution)/shard_map/pallas_call | solution.py:593
  71.9 1.9 %collective-permute-start.8 = (f32[8,256]{1,0:T(8,128)S(1)}, f32[8,256]{1,0:T(8,128)S(1)}, u32[]{:S(2)}, u32[]{:S(2)}) collective-permute-start(f32[8,256]{1,0:T(8,128)S(1)} %get-tuple-element.46), channel_id=1, source_target_pairs={{0,4},{4,0},{8,12},{12,8},{16,20},{20,16},{24,28},{28,24},{32,36},... | collective-permute-start | bytes 24584 | tf_op jit(solution)/shard_map/ppermute | solution.py:575
  73.8 2.9 %collective-permute-start.9 = (f32[8,256]{1,0:T(8,128)S(1)}, f32[8,256]{1,0:T(8,128)S(1)}, u32[]{:S(2)}, u32[]{:S(2)}) collective-permute-start(f32[8,256]{1,0:T(8,128)S(1)} %get-tuple-element.47), channel_id=1, source_target_pairs={{4,8},{8,4},{12,16},{16,12},{20,24},{24,20},{28,32},{32,28},{36,40... | collective-permute-start | bytes 24584 | tf_op jit(solution)/shard_map/ppermute | solution.py:574
  76.7 0.0 collective-permute-done.8.refs_1_
  76.7 5.4 %collective-permute-done.9.refs_2_ = f32[8,256]{1,0:T(8,128)S(1)} collective-permute-done((f32[8,256]{1,0:T(8,128)S(1)}, f32[8,256]{1,0:T(8,128)S(1)}, u32[]{:S(2)}, u32[]{:S(2)}) %collective-permute-start.9) | collective-permute-done | bytes 8224 | tf_op jit(solution)/shard_map/ppermute | solution.py:574
  82.1 4.4 %shard_map.83 = (f32[784,256]{1,0:T(8,128)S(1)}, f32[8,256]{1,0:T(8,128)S(1)}, f32[8,256]{1,0:T(8,128)S(1)}) custom-call(s32[4]{0:T(128)S(1)} %pad_add_fusion.sm_ref.refs_0_, f32[8,256]{1,0:T(8,128)S(1)} %collective-permute-done.8.refs_1_, f32[8,256]{1,0:T(8,128)S(1)} %collective-permute-done.9.refs_2_, f32[656,256]{1,0:T(8,128)S(1)} %get-tuple-element.32.c_ref.refs_3_, ...), custom_call_target="tpu_custom_call" | custom-call | flops 2000000000 | bytes 1048576 | tf_op jit(solution)/shard_map/pallas_call | solution.py:593
  86.6 1.9 %collective-permute-start.10 = (f32[8,256]{1,0:T(8,128)S(1)}, f32[8,256]{1,0:T(8,128)S(1)}, u32[]{:S(2)}, u32[]{:S(2)}) collective-permute-start(f32[8,256]{1,0:T(8,128)S(1)} %get-tuple-element.49), channel_id=1, source_target_pairs={{0,4},{4,0},{8,12},{12,8},{16,20},{20,16},{24,28},{28,24},{32,36},... | collective-permute-start | bytes 24584 | tf_op jit(solution)/shard_map/ppermute | solution.py:575
  88.5 2.9 %collective-permute-start.11 = (f32[8,256]{1,0:T(8,128)S(1)}, f32[8,256]{1,0:T(8,128)S(1)}, u32[]{:S(2)}, u32[]{:S(2)}) collective-permute-start(f32[8,256]{1,0:T(8,128)S(1)} %get-tuple-element.50), channel_id=1, source_target_pairs={{4,8},{8,4},{12,16},{16,12},{20,24},{24,20},{28,32},{32,28},{36,40... | collective-permute-start | bytes 24584 | tf_op jit(solution)/shard_map/ppermute | solution.py:574
  91.4 0.0 collective-permute-done.10.ra_ref
  91.4 5.4 %collective-permute-done.11.rb_ref = f32[8,256]{1,0:T(8,128)S(1)} collective-permute-done((f32[8,256]{1,0:T(8,128)S(1)}, f32[8,256]{1,0:T(8,128)S(1)}, u32[]{:S(2)}, u32[]{:S(2)}) %collective-permute-start.11) | collective-permute-done | bytes 8224 | tf_op jit(solution)/shard_map/ppermute | solution.py:574
  96.8 2.8 %shard_map.84 = (f32[64,256]{1,0:T(8,128)}, f32[64,256]{1,0:T(8,128)}) custom-call(s32[4]{0:T(128)S(1)} %pad_add_fusion.sm_ref.refs_0_, f32[8,256]{1,0:T(8,128)S(1)} %collective-permute-done.10.ra_ref, f32[8,256]{1,0:T(8,128)S(1)} %collective-permute-done.11.rb_ref, f32[656,256]{1,0:T(8,128)S(1)} %get-tuple-element.32.c_ref.refs_3_, ...), custom_call_target="tpu_custom_call" | custom-call | flops 2000000000 | bytes 1048576 | tf_op jit(solution)/shard_map/pallas_call | solution.py:597
Async XLA Ops:
  2.4 12.4 %all-to-all-start = ((f32[4,96,256]{2,1,0:T(8,128)}), f32[4,96,256]{2,1,0:T(8,128)S(1)}, u32[]{:S(2)}, u32[]{:S(2)}) async-start(f32[4,96,256]{2,1,0:T(8,128)} %shard_map.77), calls=%async_computation | async-start | bytes 786432 | tf_op jit(solution)/shard_map/all_to_all | solution.py:545
  15.3 17.0 %collective-permute-start.2 = (f32[16,256]{1,0:T(8,128)S(1)}, f32[16,256]{1,0:T(8,128)S(1)}, u32[]{:S(2)}, u32[]{:S(2)}) collective-permute-start(f32[16,256]{1,0:T(8,128)S(1)} %get-tuple-element.30), channel_id=1, source_target_pairs={{8,0},{12,4},{16,8},{20,12},{24,16},{28,20},{32,24},{36,28},{40,32... | collective-permute-start | bytes 49160 | tf_op jit(solution)/shard_map/ppermute | solution.py:548
  21.9 10.4 %collective-permute-start.3 = (f32[16,256]{1,0:T(8,128)S(1)}, f32[16,256]{1,0:T(8,128)S(1)}, u32[]{:S(2)}, u32[]{:S(2)}) collective-permute-start(f32[16,256]{1,0:T(8,128)S(1)} %get-tuple-element.31), channel_id=1, source_target_pairs={{12,0},{16,4},{20,8},{24,12},{28,16},{32,20},{36,24},{40,28},{44,3... | collective-permute-start | bytes 49160 | tf_op jit(solution)/shard_map/ppermute | solution.py:548
  23.8 8.5 %collective-permute-start = (f32[40,256]{1,0:T(8,128)S(1)}, f32[40,256]{1,0:T(8,128)S(1)}, u32[]{:S(2)}, u32[]{:S(2)}) collective-permute-start(f32[40,256]{1,0:T(8,128)S(1)} %get-tuple-element.28), channel_id=1, source_target_pairs={{0,4},{4,0},{8,12},{12,8},{16,20},{20,16},{24,28},{28,24},{32,36},... | collective-permute-start | bytes 122888 | tf_op jit(solution)/shard_map/ppermute | solution.py:567
  27.2 8.6 %collective-permute-start.1 = (f32[40,256]{1,0:T(8,128)S(1)}, f32[40,256]{1,0:T(8,128)S(1)}, u32[]{:S(2)}, u32[]{:S(2)}) collective-permute-start(f32[40,256]{1,0:T(8,128)S(1)} %get-tuple-element.29), channel_id=1, source_target_pairs={{0,764},{4,8},{8,4},{12,16},{16,12},{20,24},{24,20},{28,32},{32,28... | collective-permute-start | bytes 122888 | tf_op jit(solution)/shard_map/ppermute | solution.py:564
  42.6 4.8 %collective-permute-start.4 = (f32[8,256]{1,0:T(8,128)S(1)}, f32[8,256]{1,0:T(8,128)S(1)}, u32[]{:S(2)}, u32[]{:S(2)}) collective-permute-start(f32[8,256]{1,0:T(8,128)S(1)} %get-tuple-element.34), channel_id=1, source_target_pairs={{0,4},{4,0},{8,12},{12,8},{16,20},{20,16},{24,28},{28,24},{32,36},... | collective-permute-start | bytes 24584 | tf_op jit(solution)/shard_map/ppermute | solution.py:575
  44.5 8.3 %collective-permute-start.5 = (f32[8,256]{1,0:T(8,128)S(1)}, f32[8,256]{1,0:T(8,128)S(1)}, u32[]{:S(2)}, u32[]{:S(2)}) collective-permute-start(f32[8,256]{1,0:T(8,128)S(1)} %get-tuple-element.35), channel_id=1, source_target_pairs={{4,8},{8,4},{12,16},{16,12},{20,24},{24,20},{28,32},{32,28},{36,40... | collective-permute-start | bytes 24584 | tf_op jit(solution)/shard_map/ppermute | solution.py:574
  57.3 4.8 %collective-permute-start.6 = (f32[8,256]{1,0:T(8,128)S(1)}, f32[8,256]{1,0:T(8,128)S(1)}, u32[]{:S(2)}, u32[]{:S(2)}) collective-permute-start(f32[8,256]{1,0:T(8,128)S(1)} %get-tuple-element.43), channel_id=1, source_target_pairs={{0,4},{4,0},{8,12},{12,8},{16,20},{20,16},{24,28},{28,24},{32,36},... | collective-permute-start | bytes 24584 | tf_op jit(solution)/shard_map/ppermute | solution.py:575
  59.2 8.3 %collective-permute-start.7 = (f32[8,256]{1,0:T(8,128)S(1)}, f32[8,256]{1,0:T(8,128)S(1)}, u32[]{:S(2)}, u32[]{:S(2)}) collective-permute-start(f32[8,256]{1,0:T(8,128)S(1)} %get-tuple-element.44), channel_id=1, source_target_pairs={{4,8},{8,4},{12,16},{16,12},{20,24},{24,20},{28,32},{32,28},{36,40... | collective-permute-start | bytes 24584 | tf_op jit(solution)/shard_map/ppermute | solution.py:574
  71.9 4.8 %collective-permute-start.8 = (f32[8,256]{1,0:T(8,128)S(1)}, f32[8,256]{1,0:T(8,128)S(1)}, u32[]{:S(2)}, u32[]{:S(2)}) collective-permute-start(f32[8,256]{1,0:T(8,128)S(1)} %get-tuple-element.46), channel_id=1, source_target_pairs={{0,4},{4,0},{8,12},{12,8},{16,20},{20,16},{24,28},{28,24},{32,36},... | collective-permute-start | bytes 24584 | tf_op jit(solution)/shard_map/ppermute | solution.py:575
  73.8 8.3 %collective-permute-start.9 = (f32[8,256]{1,0:T(8,128)S(1)}, f32[8,256]{1,0:T(8,128)S(1)}, u32[]{:S(2)}, u32[]{:S(2)}) collective-permute-start(f32[8,256]{1,0:T(8,128)S(1)} %get-tuple-element.47), channel_id=1, source_target_pairs={{4,8},{8,4},{12,16},{16,12},{20,24},{24,20},{28,32},{32,28},{36,40... | collective-permute-start | bytes 24584 | tf_op jit(solution)/shard_map/ppermute | solution.py:574
  86.6 4.8 %collective-permute-start.10 = (f32[8,256]{1,0:T(8,128)S(1)}, f32[8,256]{1,0:T(8,128)S(1)}, u32[]{:S(2)}, u32[]{:S(2)}) collective-permute-start(f32[8,256]{1,0:T(8,128)S(1)} %get-tuple-element.49), channel_id=1, source_target_pairs={{0,4},{4,0},{8,12},{12,8},{16,20},{20,16},{24,28},{28,24},{32,36},... | collective-permute-start | bytes 24584 | tf_op jit(solution)/shard_map/ppermute | solution.py:575
  88.5 8.3 %collective-permute-start.11 = (f32[8,256]{1,0:T(8,128)S(1)}, f32[8,256]{1,0:T(8,128)S(1)}, u32[]{:S(2)}, u32[]{:S(2)}) collective-permute-start(f32[8,256]{1,0:T(8,128)S(1)} %get-tuple-element.50), channel_id=1, source_target_pairs={{4,8},{8,4},{12,16},{16,12},{20,24},{24,20},{28,32},{32,28},{36,40... | collective-permute-start | bytes 24584 | tf_op jit(solution)/shard_map/ppermute | solution.py:574

commit v2 on v1

--- a/solution.py
+++ b/solution.py
@@ -49,6 +49,11 @@
 
 
 def loop(count, body, unroll):
+    if unroll >= count:
+        for k in range(count):
+            body(k)
+        return
+
     def step(i, carry):
         for k in range(unroll):
             body(i * unroll + k)
@@ -125,15 +130,17 @@
 
 
 def phase_one(step, c_ref, d_ref, bd_ref, wf_ref, wb_ref, s_in, s_out, v_ref, v2_ref, xp_ref, ext_ref,
-              sm_ref, a_ref, b_ref):
+              sm_ref, a_ref, b_ref, beside=(), unroll=16):
     alpha, beta = step
 
     def forward(n):
         rows = blk(n)
         value = d_ref[blk(n, D_WGT), :] * s_out[blk(n, S_R), :]
         v2_ref[rows, :] = apply_weights(value, wf_ref, n)
-
-    loop(16, forward, 8)
+        for work in beside[:1]:
+            work(n)
+
+    loop(16, forward, unroll)
     for t in range(4):
         h = apply_blocks(bd_ref, 0, v2_ref[t * 64 : t * 64 + 64, :], t)
         h = h * d_ref[D_RD + t * 64 : D_RD + t * 64 + 64, :]
@@ -142,7 +149,7 @@
     def backward(n):
         v_ref[blk(n), :] = c_ref[blk(n, C_ACT), :] * apply_weights(v2_ref[blk(n), :], wb_ref, n)
 
-    loop(16, backward, 8)
+    loop(16, backward, unroll)
     ext_ref[...] = jnp.zeros((8, PL), F32)
 
     def update(n, z):
@@ -219,7 +226,7 @@
         q = v2_ref[rows, :] + apply_weights(s_out[blk(n, S_U), :], m_ref, n)
         v_ref[rows, :] = c_ref[blk(n, C_ACT), :] * q
 
-    loop(16, local, 8)
+    loop(16, local, 16)
 
     def update(n, z):
         s_out[blk(n, S_R), :] = s_in[blk(n, S_R), :] - z
@@ -258,8 +265,8 @@
 
 def store_pair(w_ref, n, j, value):
     high, low = split(value)
-    w_ref[pl.ds(pl.multiple_of(n * 512 + j * NB, 16), NB), :] = high
-    w_ref[pl.ds(pl.multiple_of(n * 512 + 256 + j * NB, 16), NB), :] = low
+    w_ref[blk(n * 32 + j), :] = high
+    w_ref[blk(n * 32 + 16 + j), :] = low
 
 
 def build_sums(m_ref, count, ta_ref, tb_ref):
@@ -378,7 +385,8 @@
 
 
 def first_kernel(sm_ref, g_ref, ra_ref, rb_ref, t2_ref, t3_ref, c_ref, m_ref, d_ref, bd_ref, wf_ref, wb_ref, mg_ref, s_ref, a_ref,
-                 b_ref, v_ref, v2_ref, xp_ref, ext_ref, p_ref, ta_ref, tb_ref, h_ref, f_ref):
+                 b_ref, v_ref, v2_ref, xp_ref, ext_ref, p_ref, ta_ref, tb_ref, h_ref, f_ref, tc_ref,
+                 td_ref):
     even = jnp.full((F_ROWS, PL), sm_ref[0], jnp.int32) == 0
     rec_a, rec_b = ra_ref[...], rb_ref[...]
     f_ref[0] = jnp.where(even, rec_b, rec_a)
@@ -457,22 +465,22 @@
     s_ref[S_X : S_X + 256, :] = jnp.zeros((256, PL), F32)
     s_ref[S_GU : S_GU + 8, :] = jnp.zeros((8, PL), F32)
 
-    def product(w_ref, mask, hot_y, hot_z):
+    def product(w_ref, y_ref, z_ref, mask, hot_y, hot_z):
         for start, part in expand(p_ref, basis(1), mask, hot_y):
-            ta_ref[start : start + 128, :] = part
+            y_ref[start : start + 128, :] = part
         for start, part in expand(p_ref, basis(2), mask, hot_z):
-            tb_ref[start : start + 128, :] = part
+            z_ref[start : start + 128, :] = part
 
         def build(n):
-            ty = ta_ref[blk(n), :]
-            tz = tb_ref[blk(n), :]
+            ty = y_ref[blk(n), :]
+            tz = z_ref[blk(n), :]
             for b in range(NB):
                 store_pair(w_ref, n, b, ty[b : b + 1, :] * tz)
 
-        loop(16, build, 2)
-
-    product(wf_ref, by_row, e1, e2)
-    product(wb_ref, by_col, e3, e4)
+        return build
+
+    loop(16, product(wf_ref, ta_ref, tb_ref, by_row, e1, e2), 2)
+    build_second = product(wb_ref, tc_ref, td_ref, by_col, e3, e4)
 
     def ghost_list(r):
         return [f_ref[side, t * F_STEP + r : t * F_STEP + r + 1, :]
@@ -484,7 +492,7 @@
         tb_ref[start : start + 128, :] = part
     build_sums(mg_ref, 8, ta_ref, tb_ref)
     phase_one(STEPS[0], c_ref, d_ref, bd_ref, wf_ref, wb_ref, s_ref, s_ref, v_ref, v2_ref, xp_ref,
-              ext_ref, sm_ref, a_ref, b_ref)
+              ext_ref, sm_ref, a_ref, b_ref, beside=(build_second,))
 
 
 def middle_kernel(k, sm_ref, ra_ref, rb_ref, c_ref, d_ref, bd_ref, bk_ref, wf_ref, wb_ref, m_ref,
@@ -582,7 +590,7 @@
         7,
         [struct(D_ROWS), struct(1024, BF16), struct(16 * 512, BF16), struct(16 * 512, BF16),
          struct(8 * 512, BF16), struct(S_ROWS), message, message],
-        WORK + [wide] * 3 + [pltpu.VMEM((128, PL), F32), pltpu.VMEM((2, F_ROWS, PL), F32)],
+        WORK + [wide] * 3 + [pltpu.VMEM((128, PL), F32), pltpu.VMEM((2, F_ROWS, PL), F32), wide, wide],
     )(scalars, slab, ra, rb, t2, t3, consts, w_m)
     for k in range(3):
         ra, rb = exchange(a, b)

time: 100 us -> 95.6 us (0.956)
  Pallas kernels: 27.3 us -> 22.8 us
    pallas_call x3, Pallas kernels: 13.3 us -> 10.4 us  [per_device(): call(kernel, 1, 11, [struct(S_ROWS), message, message], WORK)]
    pallas_call x1, Pallas kernels: 6.73 us -> 5.39 us  [per_device(): call(first_kernel, 1, 7, [struct(D_ROWS), struct(1024, BF16), struct(16 *...]
where the time goes in v2:
time: 95.6 us; the launch traced here: 95 us
  starting transfers between devices  38.2 us (40%)
  waiting for transfers between devices  33.1 us (35%)
  Pallas kernels  22.8 us (24%)
    ppermute x4, waiting for transfers between devices, exchange(): rb = lax.ppermute(b, 'slab', swap_b)  21.6 us
    ppermute x4, starting transfers between devices, exchange(): rb = lax.ppermute(b, 'slab', swap_b)  11.5 us
    pallas_call x3, Pallas kernels, per_device(): call(kernel, 1, 11, [struct(S_ROWS), message, message], WORK)  10.4 us
    ppermute x2, starting transfers between devices, ahead(): lax.ppermute(block, 'slab', [((i + distance) % slabs, i) for i in range(s...  8.5 us
    all_to_all x1, waiting for transfers between devices, gather(): return lax.all_to_all(block, 'tile', 0, 0)  8 us
    ppermute x4, starting transfers between devices, exchange(): ra = lax.ppermute(a, 'slab', swap_a)  7.68 us
    pallas_call x1, Pallas kernels, per_device(): call(first_kernel, 1, 7, [struct(D_ROWS), struct(1024, BF16), struct(16 *...  5.39 us
    all_to_all x1, starting transfers between devices, gather(): return lax.all_to_all(block, 'tile', 0, 0)  4.3 us
  transfers between devices with their start and end apart: 13, of which 6 were waited for; matrix products, arithmetic and copies ran while one was open for 0% of the time, Pallas kernels for 2%

profile of v2, /device:TPU:512, one launch (start us, length us, event | category | flops | bytes accessed | tf_op | source)
XLA Modules:
  0.0 95.0 jit_solution(14244590823646241418)
XLA Ops:
  0.6 1.7 %shard_map.77 = f32[4,96,256]{2,1,0:T(8,128)} custom-call(s32[4]{0:T(128)} %ord_hbm.1, s32[4]{0:T(128)} %route_hbm.1, f32[64,256]{1,0:T(8,128)} %bitcast.7, f32[4,768]{1,0:T(4,128)} %stiff_hbm.1, f32[4,768]{1,0:T(4,128)} %table_hbm.1, f32[4,48]{1,0:T(4,128)} %eig_hbm.1), custom_call_target="tpu_custom_call" | custom-call | flops 2000000000 | bytes 1048576 | tf_op jit(solution)/shard_map/pallas_call | solution.py:558
  2.4 4.3 %all-to-all-start = ((f32[4,96,256]{2,1,0:T(8,128)}), f32[4,96,256]{2,1,0:T(8,128)S(1)}, u32[]{:S(2)}, u32[]{:S(2)}) async-start(f32[4,96,256]{2,1,0:T(8,128)} %shard_map.77), calls=%async_computation | async-start | bytes 786432 | tf_op jit(solution)/shard_map/all_to_all | solution.py:553
  6.7 0.1 pad_add_fusion.sm_ref.refs_0_
  6.7 8.0 %all-to-all-done.g_ref = f32[4,96,256]{2,1,0:T(8,128)S(1)} async-done(((f32[4,96,256]{2,1,0:T(8,128)}), f32[4,96,256]{2,1,0:T(8,128)S(1)}, u32[]{:S(2)}, u32[]{:S(2)}) %all-to-all-start) | async-done | bytes 393248 | tf_op jit(solution)/shard_map/all_to_all | solution.py:553
  14.7 0.6 shard_map.78
  15.3 6.6 %collective-permute-start.2 = (f32[16,256]{1,0:T(8,128)S(1)}, f32[16,256]{1,0:T(8,128)S(1)}, u32[]{:S(2)}, u32[]{:S(2)}) collective-permute-start(f32[16,256]{1,0:T(8,128)S(1)} %get-tuple-element.30), channel_id=1, source_target_pairs={{8,0},{12,4},{16,8},{20,12},{24,16},{28,20},{32,24},{36,28},{40,32... | collective-permute-start | bytes 49160 | tf_op jit(solution)/shard_map/ppermute | solution.py:556
  21.9 1.9 %collective-permute-start.3 = (f32[16,256]{1,0:T(8,128)S(1)}, f32[16,256]{1,0:T(8,128)S(1)}, u32[]{:S(2)}, u32[]{:S(2)}) collective-permute-start(f32[16,256]{1,0:T(8,128)S(1)} %get-tuple-element.31), channel_id=1, source_target_pairs={{12,0},{16,4},{20,8},{24,12},{28,16},{32,20},{36,24},{40,28},{44,3... | collective-permute-start | bytes 49160 | tf_op jit(solution)/shard_map/ppermute | solution.py:556
  23.8 3.4 %collective-permute-start = (f32[40,256]{1,0:T(8,128)S(1)}, f32[40,256]{1,0:T(8,128)S(1)}, u32[]{:S(2)}, u32[]{:S(2)}) collective-permute-start(f32[40,256]{1,0:T(8,128)S(1)} %get-tuple-element.28), channel_id=1, source_target_pairs={{0,4},{4,0},{8,12},{12,8},{16,20},{20,16},{24,28},{28,24},{32,36},... | collective-permute-start | bytes 122888 | tf_op jit(solution)/shard_map/ppermute | solution.py:575
  27.2 2.9 %collective-permute-start.1 = (f32[40,256]{1,0:T(8,128)S(1)}, f32[40,256]{1,0:T(8,128)S(1)}, u32[]{:S(2)}, u32[]{:S(2)}) collective-permute-start(f32[40,256]{1,0:T(8,128)S(1)} %get-tuple-element.29), channel_id=1, source_target_pairs={{0,764},{4,8},{8,4},{12,16},{16,12},{20,24},{24,20},{28,32},{32,28... | collective-permute-start | bytes 122888 | tf_op jit(solution)/shard_map/ppermute | solution.py:572
  30.1 2.2 %shard_map.79 = (f32[656,256]{1,0:T(8,128)S(1)}, bf16[512,256]{1,0:T(8,128)(2,1)S(1)}, bf16[8192,256]{1,0:T(8,128)(2,1)S(1)}) custom-call(s32[4]{0:T(128)S(1)} %pad_add_fusion.sm_ref.refs_0_, f32[4,96,256]{2,1,0:T(8,128)S(1)} %all-to-all-done.g_ref), custom_call_target="tpu_custom_call" | custom-call | flops 2000000000 | bytes 1048576 | tf_op jit(solution)/shard_map/pallas_call | solution.py:576
  32.3 0.0 collective-permute-done.2.t2_ref
  32.3 0.0 collective-permute-done.3.t3_ref
  32.3 0.0 collective-permute-done.ra_ref
  32.3 3.5 %collective-permute-done.1.rb_ref = f32[40,256]{1,0:T(8,128)S(1)} collective-permute-done((f32[40,256]{1,0:T(8,128)S(1)}, f32[40,256]{1,0:T(8,128)S(1)}, u32[]{:S(2)}, u32[]{:S(2)}) %collective-permute-start.1) | collective-permute-done | bytes 40992 | tf_op jit(solution)/shard_map/ppermute | solution.py:572
  35.9 5.4 %shard_map.80 = (f32[552,256]{1,0:T(8,128)S(1)}, bf16[1024,256]{1,0:T(8,128)(2,1)S(1)}, bf16[8192,256]{1,0:T(8,128)(2,1)S(1)}, bf16[8192,256]{1,0:T(8,128)(2,1)S...) custom-call(s32[4]{0:T(128)S(1)} %pad_add_fusion.sm_ref.refs_0_, ...), custom_call_target="tpu_custom_call" | custom-call | flops 2000000000 | bytes 1048576 | tf_op jit(solution)/shard_map/pallas_call | solution.py:587
  41.3 1.9 %collective-permute-start.4 = (f32[8,256]{1,0:T(8,128)S(1)}, f32[8,256]{1,0:T(8,128)S(1)}, u32[]{:S(2)}, u32[]{:S(2)}) collective-permute-start(f32[8,256]{1,0:T(8,128)S(1)} %get-tuple-element.34), channel_id=1, source_target_pairs={{0,4},{4,0},{8,12},{12,8},{16,20},{20,16},{24,28},{28,24},{32,36},... | collective-permute-start | bytes 24584 | tf_op jit(solution)/shard_map/ppermute | solution.py:583
  43.2 2.9 %collective-permute-start.5 = (f32[8,256]{1,0:T(8,128)S(1)}, f32[8,256]{1,0:T(8,128)S(1)}, u32[]{:S(2)}, u32[]{:S(2)}) collective-permute-start(f32[8,256]{1,0:T(8,128)S(1)} %get-tuple-element.35), channel_id=1, source_target_pairs={{4,8},{8,4},{12,16},{16,12},{20,24},{24,20},{28,32},{32,28},{36,40... | collective-permute-start | bytes 24584 | tf_op jit(solution)/shard_map/ppermute | solution.py:582
  46.1 0.0 collective-permute-done.4.refs_1_
  46.1 5.4 %collective-permute-done.5.refs_2_ = f32[8,256]{1,0:T(8,128)S(1)} collective-permute-done((f32[8,256]{1,0:T(8,128)S(1)}, f32[8,256]{1,0:T(8,128)S(1)}, u32[]{:S(2)}, u32[]{:S(2)}) %collective-permute-start.5) | collective-permute-done | bytes 8224 | tf_op jit(solution)/shard_map/ppermute | solution.py:582
  51.5 3.5 %shard_map.81 = (f32[784,256]{1,0:T(8,128)S(1)}, f32[8,256]{1,0:T(8,128)S(1)}, f32[8,256]{1,0:T(8,128)S(1)}) custom-call(s32[4]{0:T(128)S(1)} %pad_add_fusion.sm_ref.refs_0_, f32[8,256]{1,0:T(8,128)S(1)} %collective-permute-done.4.refs_1_, f32[8,256]{1,0:T(8,128)S(1)} %collective-permute-done.5.refs_2_, f32[656,256]{1,0:T(8,128)S(1)} %get-tuple-element.32.c_ref.refs_3_, ...), custom_call_target="tpu_custom_call" | custom-call | flops 2000000000 | bytes 1048576 | tf_op jit(solution)/shard_map/pallas_call | solution.py:601
  54.9 1.9 %collective-permute-start.6 = (f32[8,256]{1,0:T(8,128)S(1)}, f32[8,256]{1,0:T(8,128)S(1)}, u32[]{:S(2)}, u32[]{:S(2)}) collective-permute-start(f32[8,256]{1,0:T(8,128)S(1)} %get-tuple-element.43), channel_id=1, source_target_pairs={{0,4},{4,0},{8,12},{12,8},{16,20},{20,16},{24,28},{28,24},{32,36},... | collective-permute-start | bytes 24584 | tf_op jit(solution)/shard_map/ppermute | solution.py:583
  56.9 2.9 %collective-permute-start.7 = (f32[8,256]{1,0:T(8,128)S(1)}, f32[8,256]{1,0:T(8,128)S(1)}, u32[]{:S(2)}, u32[]{:S(2)}) collective-permute-start(f32[8,256]{1,0:T(8,128)S(1)} %get-tuple-element.44), channel_id=1, source_target_pairs={{4,8},{8,4},{12,16},{16,12},{20,24},{24,20},{28,32},{32,28},{36,40... | collective-permute-start | bytes 24584 | tf_op jit(solution)/shard_map/ppermute | solution.py:582
  59.8 0.0 collective-permute-done.6.refs_1_
  59.8 5.4 %collective-permute-done.7.refs_2_ = f32[8,256]{1,0:T(8,128)S(1)} collective-permute-done((f32[8,256]{1,0:T(8,128)S(1)}, f32[8,256]{1,0:T(8,128)S(1)}, u32[]{:S(2)}, u32[]{:S(2)}) %collective-permute-start.7) | collective-permute-done | bytes 8224 | tf_op jit(solution)/shard_map/ppermute | solution.py:582
  65.2 3.4 %shard_map.82 = (f32[784,256]{1,0:T(8,128)S(1)}, f32[8,256]{1,0:T(8,128)S(1)}, f32[8,256]{1,0:T(8,128)S(1)}) custom-call(s32[4]{0:T(128)S(1)} %pad_add_fusion.sm_ref.refs_0_, f32[8,256]{1,0:T(8,128)S(1)} %collective-permute-done.6.refs_1_, f32[8,256]{1,0:T(8,128)S(1)} %collective-permute-done.7.refs_2_, f32[656,256]{1,0:T(8,128)S(1)} %get-tuple-element.32.c_ref.refs_3_, ...), custom_call_target="tpu_custom_call" | custom-call | flops 2000000000 | bytes 1048576 | tf_op jit(solution)/shard_map/pallas_call | solution.py:601
  68.6 1.9 %collective-permute-start.8 = (f32[8,256]{1,0:T(8,128)S(1)}, f32[8,256]{1,0:T(8,128)S(1)}, u32[]{:S(2)}, u32[]{:S(2)}) collective-permute-start(f32[8,256]{1,0:T(8,128)S(1)} %get-tuple-element.46), channel_id=1, source_target_pairs={{0,4},{4,0},{8,12},{12,8},{16,20},{20,16},{24,28},{28,24},{32,36},... | collective-permute-start | bytes 24584 | tf_op jit(solution)/shard_map/ppermute | solution.py:583
  70.5 2.9 %collective-permute-start.9 = (f32[8,256]{1,0:T(8,128)S(1)}, f32[8,256]{1,0:T(8,128)S(1)}, u32[]{:S(2)}, u32[]{:S(2)}) collective-permute-start(f32[8,256]{1,0:T(8,128)S(1)} %get-tuple-element.47), channel_id=1, source_target_pairs={{4,8},{8,4},{12,16},{16,12},{20,24},{24,20},{28,32},{32,28},{36,40... | collective-permute-start | bytes 24584 | tf_op jit(solution)/shard_map/ppermute | solution.py:582
  73.4 0.0 collective-permute-done.8.refs_1_
  73.4 5.4 %collective-permute-done.9.refs_2_ = f32[8,256]{1,0:T(8,128)S(1)} collective-permute-done((f32[8,256]{1,0:T(8,128)S(1)}, f32[8,256]{1,0:T(8,128)S(1)}, u32[]{:S(2)}, u32[]{:S(2)}) %collective-permute-start.9) | collective-permute-done | bytes 8224 | tf_op jit(solution)/shard_map/ppermute | solution.py:582
  78.8 3.4 %shard_map.83 = (f32[784,256]{1,0:T(8,128)S(1)}, f32[8,256]{1,0:T(8,128)S(1)}, f32[8,256]{1,0:T(8,128)S(1)}) custom-call(s32[4]{0:T(128)S(1)} %pad_add_fusion.sm_ref.refs_0_, f32[8,256]{1,0:T(8,128)S(1)} %collective-permute-done.8.refs_1_, f32[8,256]{1,0:T(8,128)S(1)} %collective-permute-done.9.refs_2_, f32[656,256]{1,0:T(8,128)S(1)} %get-tuple-element.32.c_ref.refs_3_, ...), custom_call_target="tpu_custom_call" | custom-call | flops 2000000000 | bytes 1048576 | tf_op jit(solution)/shard_map/pallas_call | solution.py:601
  82.3 1.9 %collective-permute-start.10 = (f32[8,256]{1,0:T(8,128)S(1)}, f32[8,256]{1,0:T(8,128)S(1)}, u32[]{:S(2)}, u32[]{:S(2)}) collective-permute-start(f32[8,256]{1,0:T(8,128)S(1)} %get-tuple-element.49), channel_id=1, source_target_pairs={{0,4},{4,0},{8,12},{12,8},{16,20},{20,16},{24,28},{28,24},{32,36},... | collective-permute-start | bytes 24584 | tf_op jit(solution)/shard_map/ppermute | solution.py:583
  84.2 2.9 %collective-permute-start.11 = (f32[8,256]{1,0:T(8,128)S(1)}, f32[8,256]{1,0:T(8,128)S(1)}, u32[]{:S(2)}, u32[]{:S(2)}) collective-permute-start(f32[8,256]{1,0:T(8,128)S(1)} %get-tuple-element.50), channel_id=1, source_target_pairs={{4,8},{8,4},{12,16},{16,12},{20,24},{24,20},{28,32},{32,28},{36,40... | collective-permute-start | bytes 24584 | tf_op jit(solution)/shard_map/ppermute | solution.py:582
  87.1 0.0 collective-permute-done.10.ra_ref
  87.1 5.4 %collective-permute-done.11.rb_ref = f32[8,256]{1,0:T(8,128)S(1)} collective-permute-done((f32[8,256]{1,0:T(8,128)S(1)}, f32[8,256]{1,0:T(8,128)S(1)}, u32[]{:S(2)}, u32[]{:S(2)}) %collective-permute-start.11) | collective-permute-done | bytes 8224 | tf_op jit(solution)/shard_map/ppermute | solution.py:582
  92.5 2.5 %shard_map.84 = (f32[64,256]{1,0:T(8,128)}, f32[64,256]{1,0:T(8,128)}) custom-call(s32[4]{0:T(128)S(1)} %pad_add_fusion.sm_ref.refs_0_, f32[8,256]{1,0:T(8,128)S(1)} %collective-permute-done.10.ra_ref, f32[8,256]{1,0:T(8,128)S(1)} %collective-permute-done.11.rb_ref, f32[656,256]{1,0:T(8,128)S(1)} %get-tuple-element.32.c_ref.refs_3_, ...), custom_call_target="tpu_custom_call" | custom-call | flops 2000000000 | bytes 1048576 | tf_op jit(solution)/shard_map/pallas_call | solution.py:605
Async XLA Ops:
  2.4 12.4 %all-to-all-start = ((f32[4,96,256]{2,1,0:T(8,128)}), f32[4,96,256]{2,1,0:T(8,128)S(1)}, u32[]{:S(2)}, u32[]{:S(2)}) async-start(f32[4,96,256]{2,1,0:T(8,128)} %shard_map.77), calls=%async_computation | async-start | bytes 786432 | tf_op jit(solution)/shard_map/all_to_all | solution.py:553
  15.3 17.0 %collective-permute-start.2 = (f32[16,256]{1,0:T(8,128)S(1)}, f32[16,256]{1,0:T(8,128)S(1)}, u32[]{:S(2)}, u32[]{:S(2)}) collective-permute-start(f32[16,256]{1,0:T(8,128)S(1)} %get-tuple-element.30), channel_id=1, source_target_pairs={{8,0},{12,4},{16,8},{20,12},{24,16},{28,20},{32,24},{36,28},{40,32... | collective-permute-start | bytes 49160 | tf_op jit(solution)/shard_map/ppermute | solution.py:556
  21.9 10.4 %collective-permute-start.3 = (f32[16,256]{1,0:T(8,128)S(1)}, f32[16,256]{1,0:T(8,128)S(1)}, u32[]{:S(2)}, u32[]{:S(2)}) collective-permute-start(f32[16,256]{1,0:T(8,128)S(1)} %get-tuple-element.31), channel_id=1, source_target_pairs={{12,0},{16,4},{20,8},{24,12},{28,16},{32,20},{36,24},{40,28},{44,3... | collective-permute-start | bytes 49160 | tf_op jit(solution)/shard_map/ppermute | solution.py:556
  23.8 8.5 %collective-permute-start = (f32[40,256]{1,0:T(8,128)S(1)}, f32[40,256]{1,0:T(8,128)S(1)}, u32[]{:S(2)}, u32[]{:S(2)}) collective-permute-start(f32[40,256]{1,0:T(8,128)S(1)} %get-tuple-element.28), channel_id=1, source_target_pairs={{0,4},{4,0},{8,12},{12,8},{16,20},{20,16},{24,28},{28,24},{32,36},... | collective-permute-start | bytes 122888 | tf_op jit(solution)/shard_map/ppermute | solution.py:575
  27.2 8.6 %collective-permute-start.1 = (f32[40,256]{1,0:T(8,128)S(1)}, f32[40,256]{1,0:T(8,128)S(1)}, u32[]{:S(2)}, u32[]{:S(2)}) collective-permute-start(f32[40,256]{1,0:T(8,128)S(1)} %get-tuple-element.29), channel_id=1, source_target_pairs={{0,764},{4,8},{8,4},{12,16},{16,12},{20,24},{24,20},{28,32},{32,28... | collective-permute-start | bytes 122888 | tf_op jit(solution)/shard_map/ppermute | solution.py:572
  41.3 4.8 %collective-permute-start.4 = (f32[8,256]{1,0:T(8,128)S(1)}, f32[8,256]{1,0:T(8,128)S(1)}, u32[]{:S(2)}, u32[]{:S(2)}) collective-permute-start(f32[8,256]{1,0:T(8,128)S(1)} %get-tuple-element.34), channel_id=1, source_target_pairs={{0,4},{4,0},{8,12},{12,8},{16,20},{20,16},{24,28},{28,24},{32,36},... | collective-permute-start | bytes 24584 | tf_op jit(solution)/shard_map/ppermute | solution.py:583
  43.2 8.3 %collective-permute-start.5 = (f32[8,256]{1,0:T(8,128)S(1)}, f32[8,256]{1,0:T(8,128)S(1)}, u32[]{:S(2)}, u32[]{:S(2)}) collective-permute-start(f32[8,256]{1,0:T(8,128)S(1)} %get-tuple-element.35), channel_id=1, source_target_pairs={{4,8},{8,4},{12,16},{16,12},{20,24},{24,20},{28,32},{32,28},{36,40... | collective-permute-start | bytes 24584 | tf_op jit(solution)/shard_map/ppermute | solution.py:582
  54.9 4.8 %collective-permute-start.6 = (f32[8,256]{1,0:T(8,128)S(1)}, f32[8,256]{1,0:T(8,128)S(1)}, u32[]{:S(2)}, u32[]{:S(2)}) collective-permute-start(f32[8,256]{1,0:T(8,128)S(1)} %get-tuple-element.43), channel_id=1, source_target_pairs={{0,4},{4,0},{8,12},{12,8},{16,20},{20,16},{24,28},{28,24},{32,36},... | collective-permute-start | bytes 24584 | tf_op jit(solution)/shard_map/ppermute | solution.py:583
  56.9 8.3 %collective-permute-start.7 = (f32[8,256]{1,0:T(8,128)S(1)}, f32[8,256]{1,0:T(8,128)S(1)}, u32[]{:S(2)}, u32[]{:S(2)}) collective-permute-start(f32[8,256]{1,0:T(8,128)S(1)} %get-tuple-element.44), channel_id=1, source_target_pairs={{4,8},{8,4},{12,16},{16,12},{20,24},{24,20},{28,32},{32,28},{36,40... | collective-permute-start | bytes 24584 | tf_op jit(solution)/shard_map/ppermute | solution.py:582
  68.6 4.8 %collective-permute-start.8 = (f32[8,256]{1,0:T(8,128)S(1)}, f32[8,256]{1,0:T(8,128)S(1)}, u32[]{:S(2)}, u32[]{:S(2)}) collective-permute-start(f32[8,256]{1,0:T(8,128)S(1)} %get-tuple-element.46), channel_id=1, source_target_pairs={{0,4},{4,0},{8,12},{12,8},{16,20},{20,16},{24,28},{28,24},{32,36},... | collective-permute-start | bytes 24584 | tf_op jit(solution)/shard_map/ppermute | solution.py:583
  70.5 8.3 %collective-permute-start.9 = (f32[8,256]{1,0:T(8,128)S(1)}, f32[8,256]{1,0:T(8,128)S(1)}, u32[]{:S(2)}, u32[]{:S(2)}) collective-permute-start(f32[8,256]{1,0:T(8,128)S(1)} %get-tuple-element.47), channel_id=1, source_target_pairs={{4,8},{8,4},{12,16},{16,12},{20,24},{24,20},{28,32},{32,28},{36,40... | collective-permute-start | bytes 24584 | tf_op jit(solution)/shard_map/ppermute | solution.py:582
  82.3 4.8 %collective-permute-start.10 = (f32[8,256]{1,0:T(8,128)S(1)}, f32[8,256]{1,0:T(8,128)S(1)}, u32[]{:S(2)}, u32[]{:S(2)}) collective-permute-start(f32[8,256]{1,0:T(8,128)S(1)} %get-tuple-element.49), channel_id=1, source_target_pairs={{0,4},{4,0},{8,12},{12,8},{16,20},{20,16},{24,28},{28,24},{32,36},... | collective-permute-start | bytes 24584 | tf_op jit(solution)/shard_map/ppermute | solution.py:583
  84.2 8.3 %collective-permute-start.11 = (f32[8,256]{1,0:T(8,128)S(1)}, f32[8,256]{1,0:T(8,128)S(1)}, u32[]{:S(2)}, u32[]{:S(2)}) collective-permute-start(f32[8,256]{1,0:T(8,128)S(1)} %get-tuple-element.50), channel_id=1, source_target_pairs={{4,8},{8,4},{12,16},{16,12},{20,24},{24,20},{28,32},{32,28},{36,40... | collective-permute-start | bytes 24584 | tf_op jit(solution)/shard_map/ppermute | solution.py:582
